TPU v7x, 32 devices: a whole 2x2x4 slice. The times are simulated.
32 devices in a mesh: seq: 32 (over z, y, x, core), head: 1.
Axes of the slice: x: 2, y: 2, z: 4, core: 2. Of those that a mesh axis runs over, the one named last changes fastest.
Arguments:
- hidden: bfloat16 [4096, 1024], P('seq'), may hold values from -6 to 6
- query_weight: bfloat16 [1024, 512], P(None, 'head'), may hold values from -0.1875 to 0.1875
- key_weight: bfloat16 [1024, 512], P(None, 'head'), may hold values from -0.1875 to 0.1875
- values: bfloat16 [4096, 512], P('seq', 'head'), may hold values from -6 to 6
- grad_out: bfloat16 [4096, 512], P('seq', 'head'), may hold values from -6 to 6
- random_feats: float32 [8, 64, 256], P('head'), may hold values from -4 to 4
Outputs:
- grad_hidden: float32 [4096, 1024], P('seq')
- grad_values: bfloat16 [4096, 512], P('seq', 'head')
- grad_query_weight: float32 [1024, 512], P('seq', 'head')
- grad_key_weight: float32 [1024, 512], P('seq', 'head')
All inputs are finite; a program needn't handle non-finite values.
Results may differ from a plain program's by a relative error of at most 0.0038.
Values sent between devices are 32-bit elements; how exact they have to be, the bound alone decides.
A program may use at most 64 MiB of HBM per device.

v0:
```python
import functools

import jax
import jax.numpy as jnp
from jax import lax
from jax.experimental import pallas as pl
from jax.experimental.pallas import tpu as pltpu
from jax.sharding import PartitionSpec as P

HIGHEST = lax.Precision.HIGHEST
HIGH = lax.Precision.HIGH
LANES = 128


def phase_orders(count):
    depth = count.bit_length() - 1
    middle = list(range(1, depth - 1))
    return [
        [(bit,) for bit in [0] + middle[s:] + middle[:s] + [depth - 1]] for s in range(3)
    ]


def wide_orders(count):
    depth = count.bit_length() - 1
    pairs = [tuple(range(b, min(b + 2, depth))) for b in range(1, depth, 2)]
    return [[(0,)] + pairs, [(0,)] + pairs[::-1]]


class Peers:
    def __init__(self, count):
        self.count = count
        self.depth = count.bit_length() - 1
        self.me = lax.axis_index("seq")
        self.bits = [(self.me // 2**b) % 2 for b in range(self.depth)]

    def reach(self, group):
        found = []
        for mask in range(1, 2 ** len(group)):
            index, digit, flips = self.me, 0, 0
            for j, b in enumerate(group):
                bit = self.bits[b]
                if (mask >> j) & 1:
                    index = index + (1 - 2 * bit) * 2**b
                    bit = 1 - bit
                    flips += 2**b
                digit = 2 * digit + bit
            found.append((flips, index, digit))
        return found

    def greet(self, orders):
        met = {}
        for order in orders:
            for group in order:
                for flips, index, _ in self.reach(group):
                    met[flips] = index
        barrier = pltpu.get_barrier_semaphore()
        for flips in sorted(met):
            pl.semaphore_signal(
                barrier, inc=1, device_id={"seq": met[flips]}, device_id_type=pl.DeviceIdType.MESH
            )
        pl.semaphore_wait(barrier, len(met))


def send(src, dst, sends, recvs, index):
    copy = pltpu.make_async_remote_copy(
        src_ref=src,
        dst_ref=dst,
        send_sem=sends,
        recv_sem=recvs,
        device_id={"seq": index},
        device_id_type=pl.DeviceIdType.MESH,
    )
    copy.start()
    return copy


class Halving:
    def __init__(self, peers, order, buf, recv, sends, recvs):
        self.peers, self.order = peers, order
        self.buf, self.recv, self.sends, self.recvs = buf, recv, sends, recvs
        self.offs, self.sizes = [0], [peers.count]
        for group in order:
            size = self.sizes[-1] // 2 ** len(group)
            digit = 0
            for b in group:
                digit = 2 * digit + peers.bits[b]
            self.offs.append(self.offs[-1] + digit * size)
            self.sizes.append(size)
        self.place = self.offs[-1]
        self.steps = len(order)

    def start(self, p):
        size = self.sizes[p + 1]
        base = self.peers.count - self.sizes[p]
        self.copies, self.landed = [], []
        for m, (_, index, digit) in enumerate(self.peers.reach(self.order[p])):
            slot = self.recv.at[pl.ds(base + m * size, size)]
            self.landed.append(slot)
            part = self.buf.at[pl.ds(self.offs[p] + digit * size, size)]
            self.copies.append(
                send(part, slot, self.sends.at[3 * p + m], self.recvs.at[3 * p + m], index)
            )

    def finish(self, p):
        kept = pl.ds(self.offs[p + 1], self.sizes[p + 1])
        for copy in self.copies:
            copy.wait()
        total = self.landed[0][...]
        for slot in self.landed[1:]:
            total = total + slot[...]
        self.buf[kept] += total


class Doubling:
    def __init__(self, halving, full, sends, recvs):
        self.halving, self.full, self.sends, self.recvs = halving, full, sends, recvs

    def load(self):
        place = pl.ds(self.halving.place, 1)
        self.full[place] = self.halving.buf[place]

    def start(self, p):
        h = self.halving
        owned = self.full.at[pl.ds(h.offs[p + 1], h.sizes[p + 1])]
        self.copies = [
            send(owned, owned, self.sends.at[3 * p + m], self.recvs.at[3 * p + m], index)
            for m, (_, index, _) in enumerate(h.peers.reach(h.order[p]))
        ]

    def finish(self, p):
        for copy in self.copies:
            copy.wait()


class SmallSum:
    def __init__(self, peers, order, sent, recv, sends, recvs):
        self.peers, self.order = peers, order
        self.sent, self.recv, self.sends, self.recvs = sent, recv, sends, recvs

    def start(self, p):
        self.copies = [
            send(
                self.sent.at[p],
                self.recv.at[3 * p + m],
                self.sends.at[3 * p + m],
                self.recvs.at[3 * p + m],
                index,
            )
            for m, (_, index, _) in enumerate(self.peers.reach(self.order[p]))
        ]

    def finish(self, p):
        for copy in self.copies:
            copy.wait()
        total = self.sent[p]
        for m in range(len(self.copies)):
            total = total + self.recv[3 * p + m]
        self.sent[p + 1] = total


def fill_blocks(halvings, side, rows_ref, grads_ref):
    count = halvings[0].peers.count
    block = halvings[0].buf.shape[1]
    rows = rows_ref.shape[1]
    step = min(rows, max(block, 256))
    for first in range(0, rows, step):
        part = jnp.dot(
            rows_ref[side, pl.ds(first, step), :], grads_ref[...], preferred_element_type=jnp.float32
        )
        for b in range(step // block):
            rest = first // block + b
            for s, h in enumerate(halvings):
                spot = sum(
                    ((rest >> (bit - 1)) & 1) * (count >> (p + 1))
                    for p, bit in enumerate(sum(h.order, ()))
                    if p > 0
                )
                h.buf[side * (count // 2) + spot] = part[
                    b * block : (b + 1) * block, s * LANES : (s + 1) * LANES
                ]


def comm_kernel(count, state_streams, grad_streams, *refs):
    refs = list(refs)
    take = lambda k: [refs.pop(0) for _ in range(k)]
    has_state, has_grad = state_streams > 0, grad_streams > 0
    if has_state:
        state_ref, normal_ref = take(2)
    if has_grad:
        rows_ref, grads_ref = take(2)
    if has_state:
        state_out, normal_out = take(2)
    if has_grad:
        (grad_out,) = take(1)
    if has_state:
        state_bufs, state_recvs, state_full = (take(state_streams) for _ in range(3))
        small_sent, small_recv, small_s, small_r = take(4)
    if has_grad:
        grad_bufs, grad_recvs = (take(grad_streams) for _ in range(2))
    sends, recvs = take(2)

    peers = Peers(count)
    orders, wide = phase_orders(count), wide_orders(count)
    depth, steps = peers.depth, len(wide[0])
    sums, small, outs, grads = [], [], [], []
    slot = 0
    if has_state:
        for s in range(state_streams):
            sums.append(
                Halving(peers, wide[s % 2], state_bufs[s], state_recvs[s], sends.at[slot], recvs.at[slot])
            )
            outs.append(Doubling(sums[-1], state_full[s], sends.at[slot + 1], recvs.at[slot + 1]))
            slot += 2
            state_bufs[s][...] = state_ref[:, :, s * LANES : (s + 1) * LANES]
        small.append(SmallSum(peers, wide[0], small_sent, small_recv, small_s, small_r))
        small_sent[0] = normal_ref[...]
    if has_grad:
        for s in range(grad_streams):
            order = orders[(s + state_streams) % 3]
            grads.append(Halving(peers, order, grad_bufs[s], grad_recvs[s], sends.at[slot], recvs.at[slot]))
            slot += 1

    peers.greet([h.order for h in sums + grads])
    for h in sums + small:
        h.start(0)
    if has_grad:
        core = peers.bits[0]
        fill_blocks(grads, 1 - core, rows_ref, grads_ref)
        for h in grads:
            h.start(0)
        fill_blocks(grads, core, rows_ref, grads_ref)

    def advance(step):
        for h in grads:
            if step < depth:
                h.finish(step)
            if step + 1 < depth:
                h.start(step + 1)

    done = 0
    if has_state:
        for p in range(steps):
            for h in sums + small:
                h.finish(p)
                if p + 1 < steps:
                    h.start(p + 1)
                elif h in sums:
                    gather = outs[sums.index(h)]
                    gather.load()
                    gather.start(steps - 1)
            if p > 0:
                advance(done)
                done += 1
        for p in reversed(range(steps)):
            for h in outs:
                h.finish(p)
                if p > 0:
                    h.start(p - 1)
            if p > 0:
                advance(done)
                done += 1
    for step in range(done, depth):
        advance(step)
    if has_state:
        for s in range(state_streams):
            state_out[:, :, s * LANES : (s + 1) * LANES] = state_full[s][...]
        normal_out[...] = small_sent[steps]
    for s, h in enumerate(grads):
        grad_out[:, s * LANES : (s + 1) * LANES] = h.buf[h.place]


def communicate(count, call, state=None, grad=None):
    depth = count.bit_length() - 1
    args, shapes, scratch = [], [], []
    f32 = jnp.float32
    state_streams = grad_streams = 0
    if state is not None:
        total, normal = state
        groups, head_dim, feats = total.shape
        rows = groups * head_dim // count
        args += [total.reshape(count, rows, feats), normal]
        shapes += [
            jax.ShapeDtypeStruct((count, rows, feats), f32),
            jax.ShapeDtypeStruct(normal.shape, f32),
        ]
        state_streams = feats // LANES
        scratch += [pltpu.VMEM((count, rows, LANES), f32)] * state_streams
        scratch += [pltpu.VMEM((count - 1, rows, LANES), f32)] * state_streams
        scratch += [pltpu.VMEM((count, rows, LANES), f32)] * state_streams
        scratch += [
            pltpu.VMEM((depth + 1,) + normal.shape, f32),
            pltpu.VMEM((3 * depth,) + normal.shape, f32),
            pltpu.SemaphoreType.DMA((3 * depth,)),
            pltpu.SemaphoreType.DMA((3 * depth,)),
        ]
    if grad is not None:
        rows_t, grads = grad
        block = 2 * rows_t.shape[1] // count
        cols = grads.shape[1]
        args += [rows_t, grads]
        shapes.append(jax.ShapeDtypeStruct((block, cols), f32))
        grad_streams = cols // LANES
        scratch += [pltpu.VMEM((count, block, LANES), f32)] * grad_streams
        scratch += [pltpu.VMEM((count - 1, block, LANES), f32)] * grad_streams
    slots = 2 * state_streams + grad_streams
    scratch += [pltpu.SemaphoreType.DMA((slots, 3 * depth))] * 2
    out = pl.pallas_call(
        functools.partial(comm_kernel, count, state_streams, grad_streams),
        out_shape=tuple(shapes),
        in_specs=[pl.BlockSpec(memory_space=pltpu.VMEM)] * len(args),
        out_specs=tuple([pl.BlockSpec(memory_space=pltpu.VMEM)] * len(shapes)),
        scratch_shapes=scratch,
        compiler_params=pltpu.CompilerParams(
            collective_id=call, has_side_effects=True, vmem_limit_bytes=48 * 2**20
        ),
        name=f"exchange{call}",
    )(*args)
    out = list(out)
    if state is not None:
        out[0] = out[0].reshape(total.shape)
    return out


def features(rows, table, feat_count):
    logits = jnp.einsum("tgd,gdm->gtm", rows, table, precision=HIGHEST)
    half_norm = 0.5 * jnp.sum(rows * rows, axis=2).T
    return jnp.exp(logits - half_norm[:, :, None]) * feat_count ** (-0.5)


def feature_grad(rows, feats, grads, table, feature_scale, tok_count):
    weighted = feats * grads
    back = jnp.einsum("gtm,gdm->tgd", weighted, table, precision=HIGH)
    totals = jnp.sum(weighted, axis=2).T
    result = (back - rows * totals[:, :, None]) * feature_scale
    return result.reshape(tok_count, -1).astype(jnp.bfloat16)


def back_product(grads, weight):
    return lax.dot_general(
        grads, weight, (((1,), (1,)), ((), ())), preferred_element_type=jnp.float32
    )


def shards(count, hidden, query_weight, key_weight, values, grad_out, random_feats):
    tok_count, width = hidden.shape
    group_count, head_dim, feat_count = random_feats.shape
    feature_scale = head_dim ** (-0.25)
    rows_t = hidden.T.reshape(count // 2, 2, width // count, tok_count)
    rows_t = rows_t.transpose(1, 0, 2, 3).reshape(2, width // 2, tok_count)
    query_proj = jnp.dot(hidden, query_weight, preferred_element_type=jnp.float32)
    key_proj = jnp.dot(hidden, key_weight, preferred_element_type=jnp.float32)
    query_rows = (query_proj * feature_scale).reshape(tok_count, group_count, head_dim)
    key_rows = (key_proj * feature_scale).reshape(tok_count, group_count, head_dim)
    value_rows = values.astype(jnp.float32).reshape(tok_count, group_count, head_dim)
    key_feats = features(key_rows, random_feats, feat_count)
    local_state = jnp.einsum("tgj,gtm->gjm", value_rows, key_feats, precision=HIGH)
    local_normal = jnp.sum(key_feats, axis=1)
    value_state, normalizer = communicate(count, 0, state=(local_state, local_normal))
    query_feats = features(query_rows, random_feats, feat_count)
    numerator = jnp.einsum("gtm,gjm->tgj", query_feats, value_state, precision=HIGH)
    denominator = jnp.sum(query_feats * normalizer[:, None, :], axis=2).T
    attended = numerator / denominator[:, :, None]
    upstream = grad_out.astype(jnp.float32).reshape(tok_count, group_count, head_dim)
    grad_numer = upstream / denominator[:, :, None]
    grad_denom = -jnp.sum(upstream * attended, axis=2) / denominator
    grad_qfeat = (
        jnp.einsum("tgj,gjm->gtm", grad_numer, value_state, precision=HIGH)
        + grad_denom.T[:, :, None] * normalizer[:, None, :]
    )
    part_state = jnp.einsum("gtm,tgj->gjm", query_feats, grad_numer, precision=HIGH)
    part_normal = jnp.sum(query_feats * grad_denom.T[:, :, None], axis=1)
    grad_query = feature_grad(
        query_rows, query_feats, grad_qfeat, random_feats, feature_scale, tok_count
    )
    grad_state, grad_normal, grad_query_weight = communicate(
        count, 1, state=(part_state, part_normal), grad=(rows_t, grad_query)
    )
    grad_kfeat = (
        jnp.einsum("tgj,gjm->gtm", value_rows, grad_state, precision=HIGH) + grad_normal[:, None, :]
    )
    grad_value = jnp.einsum("gtm,gjm->tgj", key_feats, grad_state, precision=HIGH)
    grad_values = grad_value.reshape(tok_count, -1).astype(jnp.bfloat16)
    grad_key = feature_grad(key_rows, key_feats, grad_kfeat, random_feats, feature_scale, tok_count)
    (grad_key_weight,) = communicate(count, 2, grad=(rows_t, grad_key))
    both_parts = back_product(grad_query, query_weight) + back_product(grad_key, key_weight)
    grad_hidden = both_parts
    return (grad_hidden, grad_values, grad_query_weight, grad_key_weight)


def solution(mesh):
    placed = (
        P("seq", None),
        P(None, "head"),
        P(None, "head"),
        P("seq", "head"),
        P("seq", "head"),
        P("head", None, None),
    )

    def local(*args):
        out = shards(mesh.shape["seq"], *args)
        if mesh.shape["head"] == 1:
            return out
        return (lax.psum(out[0], "head"),) + tuple(out[1:])

    return jax.shard_map(
        local,
        mesh=mesh,
        in_specs=placed,
        out_specs=(P("seq", None), P("seq", "head"), P("seq", "head"), P("seq", "head")),
        check_vma=False,
    )
```

profile of v0, /device:TPU:0, one launch (start us, length us, event | category | flops | bytes accessed | tf_op | source)
XLA Modules:
  0.0 103.2 jit_solution(16273467487302675319)
XLA Ops:
  0.6 1.7 %convolution_multiply_fusion = f32[128,512]{1,0:T(8,128)S(1)} fusion(bf16[128,1024]{1,0:T(8,128)(2,1)} %param.6, bf16[1024,512]{1,0:T(8,128)(2,1)} %param.8), kind=kOutput, calls=%fused_computation.20 | convolution fusion | flops 134283264 | bytes 1572864 | tf_op jit(solution)/shard_map/dot_general | solution.py:351
  2.5 0.9 copy-done.3
  3.4 1.2 %fusion.22 = (f32[8,256]{1,0:T(8,128)S(1)}, f32[8,128,256]{2,1,0:T(8,128)S(1)}) fusion(f32[8,128]{1,0:T(8,128)S(1)} %multiply_bitcast_fusion, f32[128,8,64]{0,2,1:T(8,128)S(1)} %bitcast.93, f32[8,64,256]{2,1,0:T(8,128)S(1)} %copy-done.3), kind=kOutput, calls=%fused_computation.43 | convolution fusion | flops 202110976 | bytes 1847296 | tf_op jit(solution)/shard_map/tgd,gdm->gtm/dot_general | solution.py:325
  4.7 0.3 fusion.25
  5.1 0.5 copy-done.1
  5.6 25.0 %exchange0.1 = (f32[32,16,256]{2,1,0:T(8,128)S(1)}, f32[8,256]{1,0:T(8,128)S(1)}) custom-call(f32[32,16,256]{2,1,0:T(8,128)S(1)} %bitcast.90, f32[8,256]{1,0:T(8,128)S(1)} %get-tuple-element.24.refs_1_), custom_call_target="tpu_custom_call" | custom-call | tf_op jit(solution)/shard_map/exchange0/pallas_call | solution.py:307
  30.6 0.6 broadcast_multiply_fusion
  31.2 0.3 convolution_multiply_fusion.1
  31.7 0.6 copy-done.5
  32.4 2.2 %multiply_reduce_fusion.1 = (f32[8,128]{1,0:T(8,128)S(1)}, f32[8,128,256]{2,1,0:T(8,128)S(1)}) fusion(f32[8,256]{1,0:T(8,128)S(1)} %copy-done.14, f32[8,128]{1,0:T(8,128)S(1)} %multiply_bitcast_fusion.1, f32[128,8,64]{0,2,1:T(8,128)} %bitcast.95, f32[8,64,256]{2,1,0:T(8,128)S(1)} %copy-done.3), kind=kOutput, calls=%fused_computation.27 | convolution fusion | flops 202112000 | bytes 1851392 | tf_op jit(solution)/shard_map/tgd,gdm->gtm/dot_general | solution.py:325
  34.6 1.7 %copy.23 = f32[128,512]{0,1:T(8,128)} copy(bf16[128,512]{1,0:T(8,128)(2,1)} %param.10) | data formatting | bytes 393216 | tf_op jit(solution)/shard_map/reshape | solution.py:363
  36.4 1.7 %fusion.14 = f32[128,8]{0,1:T(8,128)S(1)} fusion(f32[128,8,64]{0,2,1:T(8,128)} %bitcast.97, f32[8,64,256]{2,1,0:T(8,128)S(1)} %bitcast.88, f32[8,128,256]{2,1,0:T(8,128)S(1)} %get-tuple-element.27, f32[128,8]{0,1:T(8,128)S(1)} %bitcast.108), kind=kOutput, calls=%fused_computation.25 | convolution fusion | flops 101121024 | bytes 1843200 | tf_op jit(solution)/shard_map/gtm,gjm->tgj/dot_general | solution.py:360
  38.1 0.9 fusion.23
  39.1 0.7 fusion.12
  39.7 1.3 %fusion.26 = f32[128,1024]{1,0:T(8,128)} fusion(bf16[128,512]{0,1:T(8,128)(2,1)S(1)} %bitcast.104, bf16[1024,512]{1,0:T(8,128)(2,1)S(1)} %copy-done), kind=kOutput, calls=%fused_computation.47 | convolution fusion | flops 134217728 | bytes 1703936 | tf_op jit(solution)/shard_map/dot_general | solution.py:339
  41.0 0.5 fusion.15
  41.5 0.2 multiply_reduce_fusion.refs_1_
  41.7 0.7 copy-done.10
  42.4 0.9 copy.26
  43.3 1.0 copy.27
  44.3 1.0 copy.28.refs_3_
  45.3 29.3 %exchange1.1 = (f32[32,16,256]{2,1,0:T(8,128)S(1)}, f32[8,256]{1,0:T(8,128)S(1)}, f32[32,512]{1,0:T(8,128)S(1)}) custom-call(f32[32,16,256]{2,1,0:T(8,128)S(1)} %bitcast.87, f32[8,256]{1,0:T(8,128)S(1)} %multiply_reduce_fusion.refs_1_, bf16[2,512,128]{2,1,0:T(8,128)(2,1)S(1)} %bitcast.85, bf16[128,512]{1,0:T(8,128)(2,1)S(1)} %copy.28.refs_3_), custom_call_target="tpu_custom_call" | custom-call | tf_op jit(solution)/shard_map/exchange1/pallas_call | solution.py:307
  74.6 0.6 fusion.24
  75.2 0.4 copy-done.4
  75.6 0.7 fusion.13
  76.5 0.3 copy-done.11
  76.7 1.3 %convolution_add_fusion.2 = f32[128,1024]{1,0:T(8,128)} fusion(f32[128,1024]{1,0:T(8,128)S(1)} %copy-done.11, bf16[128,512]{0,1:T(8,128)(2,1)S(1)} %bitcast.100, bf16[1024,512]{1,0:T(8,128)(2,1)S(1)} %copy-done.7), kind=kOutput, calls=%fused_computation.10 | convolution fusion | flops 134348800 | bytes 2228224 | tf_op jit(solution)/shard_map/dot_general | solution.py:339
  78.0 0.7 convolution_convert_fusion
  78.7 0.8 copy.31
  79.6 22.3 %exchange2.1 = f32[32,512]{1,0:T(8,128)S(1)} custom-call(bf16[2,512,128]{2,1,0:T(8,128)(2,1)S(1)} %bitcast.86, bf16[128,512]{1,0:T(8,128)(2,1)S(1)} %copy.30.refs_1_), custom_call_target="tpu_custom_call" | custom-call | tf_op jit(solution)/shard_map/exchange2/pallas_call | solution.py:307
  101.9 0.6 copy.35
  102.5 0.6 copy.36
  (33 shorter events, 0.9 us)
Async XLA Ops:
  0.6 30.5 %copy-start = (bf16[1024,512]{1,0:T(8,128)(2,1)S(1)}, bf16[1024,512]{1,0:T(8,128)(2,1)}, u32[]{:S(2)}) copy-start(bf16[1024,512]{1,0:T(8,128)(2,1)} %param.7) | copy-start | bytes 3145732
  2.4 1.0 %copy-start.3 = (f32[8,64,256]{2,1,0:T(8,128)S(1)}, f32[8,64,256]{2,1,0:T(8,128)}, u32[]{:S(2)}) copy-start(f32[8,64,256]{2,1,0:T(8,128)} %param.11) | copy-start | bytes 1572868
  3.4 1.2 %copy-start.13 = (bf16[128,512]{1,0:T(8,128)(2,1)S(1)}, bf16[128,512]{1,0:T(8,128)(2,1)}, u32[]{:S(2)}) copy-start(bf16[128,512]{1,0:T(8,128)(2,1)} %param.9) | copy-start | bytes 393220
  4.6 1.0 copy-start.1
  5.6 25.6 %copy-start.9 = (bf16[128,1024]{1,0:T(8,128)(2,1)S(1)}, bf16[128,1024]{1,0:T(8,128)(2,1)}, u32[]{:S(2)}) copy-start(bf16[128,1024]{1,0:T(8,128)(2,1)} %param.6) | copy-start | bytes 786436
  31.6 0.7 copy-start.5
  31.7 0.7 copy-start.14
  36.3 1.7 %copy-start.8 = (f32[128,512]{0,1:T(8,128)S(1)}, f32[128,512]{0,1:T(8,128)}, u32[]{:S(2)}) copy-start(f32[128,512]{0,1:T(8,128)} %copy.23) | copy-start | bytes 786436
  38.1 1.0 copy-start.6
  39.7 1.3 %copy-start.12 = (bf16[128,8,64]{0,2,1:T(8,128)(2,1)}, bf16[128,8,64]{0,2,1:T(8,128)(2,1)S(1)}, u32[]{:S(2)}) copy-start(bf16[128,8,64]{0,2,1:T(8,128)(2,1)S(1)} %fusion.12) | copy-start | bytes 393220
  41.5 1.0 copy-start.10
  42.4 32.1 %copy-start.2 = (f32[8,128,256]{2,1,0:T(8,128)S(1)}, f32[8,128,256]{2,1,0:T(8,128)}, u32[]{:S(2)}) copy-start(f32[8,128,256]{2,1,0:T(8,128)} %copy-done.1) | copy-start | bytes 3145732
  74.6 1.0 %copy-start.4 = (f32[8,64,256]{2,1,0:T(8,128)S(1)}, f32[8,64,256]{2,1,0:T(8,128)}, u32[]{:S(2)}) copy-start(f32[8,64,256]{2,1,0:T(8,128)} %param.11) | copy-start | bytes 1572868
  75.2 1.3 %copy-start.7 = (bf16[1024,512]{1,0:T(8,128)(2,1)S(1)}, bf16[1024,512]{1,0:T(8,128)(2,1)}, u32[]{:S(2)}) copy-start(bf16[1024,512]{1,0:T(8,128)(2,1)} %param.8) | copy-start | bytes 3145732
  75.6 1.1 %copy-start.11 = (f32[128,1024]{1,0:T(8,128)S(1)}, f32[128,1024]{1,0:T(8,128)}, u32[]{:S(2)}) copy-start(f32[128,1024]{1,0:T(8,128)} %fusion.26) | copy-start | bytes 1572868
where the time goes:
time: 104 us; the launch traced here: 103 us
  Pallas kernels  76.5 us (74%)
  matrix products  14 us (13%)
  local copies, waits for them, and re-layouts  10.8 us (10%)
    pallas_call x3, Pallas kernels, communicate(): pl.pallas_call(functools.partial(comm_kernel, count, state_streams, grad_...  76.5 us
    unnamed x35, local copies, waits for them, and re-layouts  6.78 us
    dot_general x2, matrix products, features(): logits = jnp.einsum('tgd,gdm->gtm', rows, table, precision=HIGHEST)  3.4 us
    dot_general x2, matrix products, back_product(): lax.dot_general(grads, weight, (((1,), (1,)), ((), ())), preferred_elemen...  2.54 us

commit v1 on v0

v1 whole, which is shorter than its diff:
```python
import functools

import jax
import jax.numpy as jnp
from jax import lax
from jax.experimental import pallas as pl
from jax.experimental.pallas import tpu as pltpu
from jax.sharding import PartitionSpec as P

F32, BF16 = jnp.float32, jnp.bfloat16
LANES = 128
MESH = pl.DeviceIdType.MESH


def flipped(index, mask, stride=1):
    out, b = index, 0
    while mask >> b:
        if (mask >> b) & 1:
            bit = (index // (stride * 2**b)) % 2
            out = out + (1 - 2 * bit) * (stride * 2**b)
        b += 1
    return out


def radices(count):
    out = []
    while count > 1:
        out.append(4 if count % 4 == 0 else 2)
        count //= out[-1]
    return out


def dot(a, b):
    return jnp.dot(a, b, preferred_element_type=F32)


def dot_t(a, b):
    return lax.dot_general(a, b, (((1,), (1,)), ((), ())), preferred_element_type=F32)


def halves(x):
    high = x.astype(BF16)
    return high, (x - high.astype(F32)).astype(BF16)


def swap(x):
    return pltpu.roll(x, LANES // 2, 1)


def remote(src, dst, send_sem, recv_sem, peer):
    return pltpu.make_async_remote_copy(
        src_ref=src, dst_ref=dst, send_sem=send_sem, recv_sem=recv_sem,
        device_id={"seq": peer}, device_id_type=MESH,
    )


def kernel(
    n, hid, wq, wk, val, gout, rf, o_hid, o_val, o_gq, o_gk,
    hid_f, hid_r, kv_s, kv_a, qg_s, qg_a, rfs, rbs, feat_k, feat_q, bwd_x,
    ar_s, ar_r, pq_s, pq_r, pk_s, pk_r, dq_p, dk_p, gv_p, dq_a, dk_a, gv_a, gw_s, gw_r,
    a2a_ss, a2a_rs, ar_ss, ar_rs, pair_ss, pair_rs, back_ss, back_rs, gw_ss, gw_rs, loc_s,
):
    groups, head_dim, feats = rf.shape
    toks, width = hid.shape
    half = width // 2
    pairs = groups // 2
    scale = head_dim ** (-0.25)
    norm = feats ** (-0.5)
    me = lax.axis_index("seq")
    mine = me % groups
    core = me % 2
    pair = mine // 2
    first = core == 0
    phases = radices(n // groups)

    barrier = pltpu.get_barrier_semaphore()

    def greet(step, carry):
        pl.semaphore_signal(
            barrier, inc=1, device_id={"seq": (me + step) % n}, device_id_type=MESH
        )
        return carry

    lax.fori_loop(1, n, greet, 0)

    def low(shape):
        return lax.broadcasted_iota(jnp.int32, shape, 1) < head_dim

    def pack(proj, other, out):
        for p in range(pairs):
            a = proj[:, p * LANES : (p + 1) * LANES]
            b = other[:, p * LANES : (p + 1) * LANES].astype(F32)
            mask = low(a.shape)
            out[2 * p] = jnp.where(mask, a, swap(b))
            out[2 * p + 1] = jnp.where(mask, swap(a), b)

    def scatter(which, sent, got):
        copies = []
        for m in range(1, groups):
            to = flipped(me, m)
            copy = remote(
                sent.at[to % groups], got.at[m], a2a_ss.at[which, m], a2a_rs.at[which, m], to
            )
            copy.start()
            copies.append(copy)
        got[0] = sent[mine]
        return copies

    pack(dot(hid[...], wk[...]) * scale, val[...], kv_s)
    pl.semaphore_wait(barrier, n - 1)
    kv_copies = scatter(0, kv_s, kv_a)
    pack(dot(hid[...], wq[...]) * scale, gout[...], qg_s)
    qg_copies = scatter(1, qg_s, qg_a)
    hid_f[0] = hid[:, :half].astype(F32)
    hid_f[1] = hid[:, half:].astype(F32)
    hid_copies = []
    for m in range(1, groups):
        to = flipped(me, m)
        copy = remote(hid_f.at[to % 2], hid_r.at[m - 1], a2a_ss.at[2, m], a2a_rs.at[2, m], to)
        copy.start()
        hid_copies.append(copy)

    rf_high, rf_low = halves(rf[mine])
    rfs[...] = jnp.concatenate([rf_high, rf_high, rf_low, rf_low], axis=0)
    rbs[...] = jnp.concatenate([rf_high, rf_low], axis=0)

    def features(x):
        rows = jnp.where(low(x.shape), x, 0.0)
        high = rows.astype(BF16).astype(F32)
        both = (high + swap(rows - high)).astype(BF16)
        logits = dot(jnp.concatenate([both, both], axis=1), rfs[...])
        return jnp.exp(logits - 0.5 * jnp.sum(rows * rows, axis=1, keepdims=True)) * norm

    def chunk(ref, c):
        return ref[2 * c : 2 * c + 2].reshape(2 * toks, ref.shape[2])

    def all_reduce(which, total):
        stride, slot = groups, 0
        for f, radix in enumerate(phases):
            ar_s[which, f] = total
            copies = []
            for d in range(1, radix):
                copy = remote(
                    ar_s.at[which, f], ar_r.at[which, f, d - 1],
                    ar_ss.at[which, f, d], ar_rs.at[which, f, d], flipped(me, d, stride),
                )
                copy.start()
                copies.append(copy)
            yield
            for d, copy in enumerate(copies):
                copy.wait()
                total = total + ar_r[which, f, d]
            stride *= radix
        summed = jnp.concatenate(
            [jnp.broadcast_to(total[7:8], (head_dim, feats)), total[8:]], axis=0
        )
        yield halves(summed)

    def finish(steps):
        for got in steps:
            if got is not None:
                return got

    lead = head_dim - 8

    total = jnp.zeros((LANES, feats), F32)
    for c in range(pairs):
        for m in (2 * c, 2 * c + 1):
            if m > 0:
                kv_copies[m - 1].wait()
        x = chunk(kv_a, c)
        b = features(x)
        feat_k[c] = b
        high, rest = halves(b)
        ones = jnp.where(low(x.shape), 1.0, x).T.astype(BF16)
        total = total + dot(ones, high) + dot(ones, rest)
    reduce_k = all_reduce(0, total[lead:])
    next(reduce_k)

    for c in range(pairs):
        for m in (2 * c, 2 * c + 1):
            if m > 0:
                qg_copies[m - 1].wait()
        feat_q[c] = features(chunk(qg_a, c))

    st_high, st_low = finish(reduce_k)
    st_both = jnp.concatenate([st_high, st_low], axis=0)
    total = jnp.zeros((LANES, feats), F32)
    for c in range(pairs):
        x = chunk(qg_a, c)
        high, rest = halves(feat_q[c])
        nd = dot_t(high, st_both)
        nd = nd[:, :LANES] + nd[:, LANES:] + dot_t(rest, st_high)
        mask = low(nd.shape)
        den = jnp.where(mask, nd, swap(nd))
        upstream = jnp.where(mask, 0.0, x) / den
        grad_den = -jnp.sum(upstream * nd / den, axis=1, keepdims=True)
        lane = lax.broadcasted_iota(jnp.int32, nd.shape, 1)
        xg = jnp.where(lane == head_dim - 1, grad_den, upstream)
        bwd_x[c] = xg
        turned_high, turned_low = halves(xg.T)
        total = total + dot(turned_high, high) + dot(turned_low, high) + dot(turned_high, rest)
    reduce_q = all_reduce(1, total[lead:])
    next(reduce_q)

    def feature_grad(x, weighted):
        high, rest = halves(weighted)
        back = dot_t(high, rbs[...]) + dot_t(rest, rbs[...])
        back = back + swap(back)
        out = (back - x * jnp.sum(weighted, axis=1, keepdims=True)) * scale
        return jnp.where(low(x.shape), out.astype(BF16).astype(F32), 0.0)

    for c in range(pairs):
        x = chunk(qg_a, c)
        high, rest = halves(bwd_x[c])
        grads = dot(
            jnp.concatenate([high, rest], axis=1), jnp.concatenate([st_high, st_high], axis=0)
        ) + dot(high, st_low)
        out = feature_grad(x, feat_q[c] * grads)
        placed = jnp.where(first, out, swap(out))
        pq_s[2 * c] = placed[:toks]
        pq_s[2 * c + 1] = placed[toks:]
    partner = flipped(me, 1)
    pq_copy = remote(pq_s, pq_r, pair_ss.at[0], pair_rs.at[0], partner)
    pq_copy.start()

    def give_back(which, sent, got):
        copies = []
        for m in range(2, groups, 2):
            copy = remote(
                sent.at[m], got.at[pair], back_ss.at[which, m], back_rs.at[which, m], flipped(me, m)
            )
            copy.start()
            copies.append(copy)
        got[pair] = sent[0]
        return copies

    pq_copy.wait()
    for m in range(groups):
        dq_p[m] = pq_s[m] + pq_r[m ^ 1]
    dq_copies = give_back(0, dq_p, dq_a)

    gs_high, gs_low = finish(reduce_q)
    gs_both = jnp.concatenate([gs_high, gs_low], axis=0)
    for c in range(pairs):
        x = chunk(kv_a, c)
        mask = low(x.shape)
        lane = lax.broadcasted_iota(jnp.int32, x.shape, 1)
        xv = jnp.where(mask, jnp.where(lane == head_dim - 1, 1.0, 0.0), x).astype(BF16)
        b = feat_k[c]
        grads = dot(jnp.concatenate([xv, xv], axis=1), gs_both)
        out = feature_grad(x, b * grads)
        high, rest = halves(b)
        gv = dot_t(high, gs_both)
        gv = gv[:, :LANES] + gv[:, LANES:] + dot_t(rest, gs_high)
        packed = jnp.where(mask, out, gv)
        pk_s[2 * c] = packed[:toks]
        pk_s[2 * c + 1] = packed[toks:]
    pk_copy = remote(pk_s, pk_r, pair_ss.at[1], pair_rs.at[1], partner)
    pk_copy.start()

    for copy in hid_copies:
        copy.wait()

    owner_half = me // (n // 2)

    def weight_sends(which, grads_p):
        total = jnp.zeros((LANES, half), F32)
        for m in range(groups):
            rows = hid_f[core] if m == 0 else hid_r[m - 1]
            total = total + dot(grads_p[m].T.astype(BF16), rows.astype(BF16))
        gw_s[which] = total.T.reshape(gw_s.shape[1:])

        def start(i, carry):
            to = core * (n // 2) + i

            @pl.when(to != me)
            def _():
                remote(
                    gw_s.at[which, i], gw_r.at[which, me // 2],
                    gw_ss.at[which, i], gw_rs.at[which, me // 2], to,
                ).start()

            @pl.when(to == me)
            def _():
                pltpu.make_async_copy(
                    gw_s.at[which, i], gw_r.at[which, me // 2], loc_s.at[which]
                ).start()

            return carry

        lax.fori_loop(0, n // 2, start, 0)

    def weight_waits(which, out):
        def wait(i, carry):
            to = core * (n // 2) + i
            source = 2 * i + owner_half
            here = remote(
                gw_s.at[which, i], gw_r.at[which, i], gw_ss.at[which, i], gw_rs.at[which, i], partner
            )

            @pl.when(to != me)
            def _():
                here.wait_send()

            @pl.when(to == me)
            def _():
                pltpu.make_async_copy(
                    gw_s.at[which, i], gw_r.at[which, me // 2], loc_s.at[which]
                ).wait()

            @pl.when(source != me)
            def _():
                here.wait_recv()

            return carry

        lax.fori_loop(0, n // 2, wait, 0)
        for p in range(pairs):
            total = gw_r[which, p]
            for i in range(p + pairs, n // 2, pairs):
                total = total + gw_r[which, i]
            out[:, p * LANES : (p + 1) * LANES] = total

    weight_sends(0, dq_p)

    pk_copy.wait()
    for m in range(groups):
        own, theirs = pk_s[m], pk_r[m ^ 1]
        one = jnp.where(first, own, theirs)
        two = jnp.where(first, theirs, own)
        mask = low(own.shape)
        dk_p[m] = jnp.where(mask, one, swap(two))
        gv_p[m] = jnp.where(mask, swap(one), two)
    weight_sends(1, dk_p)
    dk_copies = give_back(1, dk_p, dk_a)
    gv_copies = give_back(2, gv_p, gv_a)

    def joined(ref):
        return jnp.concatenate([ref[p] for p in range(pairs)], axis=1).astype(BF16)

    for copy in dq_copies:
        copy.wait()
    for copy in dk_copies:
        copy.wait()
    o_hid[...] = dot_t(joined(dq_a), wq[...]) + dot_t(joined(dk_a), wk[...])
    for copy in gv_copies:
        copy.wait()
    o_val[...] = joined(gv_a)
    weight_waits(0, o_gq)
    weight_waits(1, o_gk)


def shards(n, hidden, query_weight, key_weight, values, grad_out, random_feats):
    toks, width = hidden.shape
    groups, head_dim, feats = random_feats.shape
    cols = groups * head_dim
    pairs = groups // 2
    block = width // n
    phases = len(radices(n // groups))
    rows = head_dim + 8
    tok_block = (groups, toks, LANES)
    scratch = [
        pltpu.VMEM((2, toks, width // 2), F32),
        pltpu.VMEM((groups - 1, toks, width // 2), F32),
        pltpu.VMEM(tok_block, F32),
        pltpu.VMEM(tok_block, F32),
        pltpu.VMEM(tok_block, F32),
        pltpu.VMEM(tok_block, F32),
        pltpu.VMEM((4 * head_dim, feats), BF16),
        pltpu.VMEM((2 * head_dim, feats), BF16),
        pltpu.VMEM((pairs, 2 * toks, feats), F32),
        pltpu.VMEM((pairs, 2 * toks, feats), F32),
        pltpu.VMEM((pairs, 2 * toks, LANES), F32),
        pltpu.VMEM((2, phases, rows, feats), F32),
        pltpu.VMEM((2, phases, 3, rows, feats), F32),
        pltpu.VMEM(tok_block, F32),
        pltpu.VMEM(tok_block, F32),
        pltpu.VMEM(tok_block, F32),
        pltpu.VMEM(tok_block, F32),
        pltpu.VMEM(tok_block, F32),
        pltpu.VMEM(tok_block, F32),
        pltpu.VMEM(tok_block, F32),
        pltpu.VMEM((pairs, toks, LANES), F32),
        pltpu.VMEM((pairs, toks, LANES), F32),
        pltpu.VMEM((pairs, toks, LANES), F32),
        pltpu.VMEM((2, n // 2, block, LANES), F32),
        pltpu.VMEM((2, n // 2, block, LANES), F32),
        pltpu.SemaphoreType.DMA((3, groups)),
        pltpu.SemaphoreType.DMA((3, groups)),
        pltpu.SemaphoreType.DMA((2, phases, 4)),
        pltpu.SemaphoreType.DMA((2, phases, 4)),
        pltpu.SemaphoreType.DMA((2,)),
        pltpu.SemaphoreType.DMA((2,)),
        pltpu.SemaphoreType.DMA((3, groups)),
        pltpu.SemaphoreType.DMA((3, groups)),
        pltpu.SemaphoreType.DMA((2, n // 2)),
        pltpu.SemaphoreType.DMA((2, n // 2)),
        pltpu.SemaphoreType.DMA((2,)),
    ]
    vmem = pl.BlockSpec(memory_space=pltpu.VMEM)
    return pl.pallas_call(
        functools.partial(kernel, n),
        out_shape=(
            jax.ShapeDtypeStruct((toks, width), F32),
            jax.ShapeDtypeStruct((toks, cols), BF16),
            jax.ShapeDtypeStruct((block, cols), F32),
            jax.ShapeDtypeStruct((block, cols), F32),
        ),
        in_specs=[vmem] * 6,
        out_specs=(vmem,) * 4,
        scratch_shapes=scratch,
        compiler_params=pltpu.CompilerParams(
            collective_id=0, has_side_effects=True, vmem_limit_bytes=56 * 2**20
        ),
        name="backward",
    )(hidden, query_weight, key_weight, values, grad_out, random_feats)


def solution(mesh):
    placed = (
        P("seq", None),
        P(None, "head"),
        P(None, "head"),
        P("seq", "head"),
        P("seq", "head"),
        P("head", None, None),
    )

    def local(*args):
        out = shards(mesh.shape["seq"], *args)
        if mesh.shape["head"] == 1:
            return out
        return (lax.psum(out[0], "head"),) + tuple(out[1:])

    return jax.shard_map(
        local,
        mesh=mesh,
        in_specs=placed,
        out_specs=(P("seq", None), P("seq", "head"), P("seq", "head"), P("seq", "head")),
        check_vma=False,
    )
```

time: 104 us -> 67.5 us (0.65)
  Pallas kernels: 76.5 us -> 62.3 us
  matrix products: 14 us -> 0 us
  local copies, waits for them, and re-layouts: 10.8 us -> 4.28 us
    pallas_call x3 -> x1, Pallas kernels: 76.5 us -> 62.3 us  [shards(): pl.pallas_call(functools.partial(kernel, n), out_shape=(jax.ShapeDtypeStr...]
    dot_general x14 -> x0, matrix products: 14 us -> none  [the longest x2 3.4 us: features(): logits = jnp.einsum('tgd,gdm->gtm', rows, table, precision=HIGHEST)]
    unnamed x35 -> x10, local copies, waits for them, and re-layouts: 6.78 us -> 4.28 us
    reshape x1 -> x0, local copies, waits for them, and re-layouts: 1.73 us -> none  [shards(): grad_out.astype(jnp.float32).reshape(tok_count, group_count, head_dim)]
    convert_element_type x2 -> x0, local copies, waits for them, and re-layouts: 1.12 us -> none  [feature_grad(): return result.reshape(tok_count, -1).astype(jnp.bfloat16)]
where the time goes in v1:
time: 67.5 us; the launch traced here: 67.2 us
  Pallas kernels  62.3 us (92%)
  local copies, waits for them, and re-layouts  4.28 us (6%)
    pallas_call x1, Pallas kernels, shards(): pl.pallas_call(functools.partial(kernel, n), out_shape=(jax.ShapeDtypeStr...  62.3 us
    unnamed x10, local copies, waits for them, and re-layouts  4.28 us

profile of v1, /device:TPU:0, one launch (start us, length us, event | category | flops | bytes accessed | tf_op | source)
XLA Modules:
  0.0 67.2 jit_solution(13432024744390288267)
XLA Ops:
  0.6 62.3 %backward.1 = (f32[128,1024]{1,0:T(8,128)}, bf16[128,512]{1,0:T(8,128)(2,1)}, f32[32,512]{1,0:T(8,128)}, f32[32,512]{1,0:T(8,128)}) custom-call(bf16[128,1024]{1,0:T(8,128)(2,1)} %hid.1, bf16[1024,512]{1,0:T(8,128)(2,1)} %wq.1, bf16[1024,512]{1,0:T(8,128)(2,1)} %wk.1, bf16[128,512]{1,0:T(8,128)(2,1)} %val.1, bf16[128,512]{1,0:T(8,128)(2,1)} %gout.1, ...), custom_call_target="tpu_custom_call" | custom-call | tf_op jit(solution)/shard_map/backward/pallas_call | solution.py:402
  62.9 0.0 copy-start
  62.9 1.9 %copy.14 = f32[128,1024]{1,0:T(8,128)} copy(f32[128,1024]{1,0:T(8,128)} %get-tuple-element.8) | data formatting | bytes 1048576
  64.9 0.0 copy-done
  64.9 0.0 copy-start.2
  64.9 0.7 copy.15
  65.5 0.2 copy-done.2
  65.7 0.0 copy-start.1
  65.7 0.6 copy.16
  66.4 0.2 copy-done.1
  66.6 0.6 copy.17
Async XLA Ops:
  62.9 1.9 %copy-start = (bf16[128,512]{1,0:T(8,128)(2,1)S(1)}, bf16[128,512]{1,0:T(8,128)(2,1)}, u32[]{:S(2)}) copy-start(bf16[128,512]{1,0:T(8,128)(2,1)} %get-tuple-element.9) | copy-start | bytes 393220
  64.9 0.9 %copy-start.2 = (f32[32,512]{1,0:T(8,128)S(1)}, f32[32,512]{1,0:T(8,128)}, u32[]{:S(2)}) copy-start(f32[32,512]{1,0:T(8,128)} %get-tuple-element.10) | copy-start | bytes 196612
  65.7 0.9 %copy-start.1 = (f32[32,512]{1,0:T(8,128)S(1)}, f32[32,512]{1,0:T(8,128)}, u32[]{:S(2)}) copy-start(f32[32,512]{1,0:T(8,128)} %get-tuple-element.11) | copy-start | bytes 196612

commit v2 on v1

--- a/solution.py
+++ b/solution.py
@@ -55,14 +55,19 @@
 
 
 def kernel(
-    n, hid, wq, wk, val, gout, rf, o_hid, o_val, o_gq, o_gk,
+    n, hid_h, wq_h, wk_h, val_h, gout_h, rf_h, o_hid, o_val, o_gq, o_gk,
+    hid, wq, wk, val, gout, rf,
     hid_f, hid_r, kv_s, kv_a, qg_s, qg_a, rfs, rbs, feat_k, feat_q, bwd_x,
-    ar_s, ar_r, pq_s, pq_r, pk_s, pk_r, dq_p, dk_p, gv_p, dq_a, dk_a, gv_a, gw_s, gw_r,
-    a2a_ss, a2a_rs, ar_ss, ar_rs, pair_ss, pair_rs, back_ss, back_rs, gw_ss, gw_rs, loc_s,
+    ar_s, ar_r, pq_s, pq_r, pk_s, pk_r, dq_p, dk_p, gv_p, turned, dq_a, dk_a, gv_a, gw_s, gw_r,
+    in_ss, a2a_ss, a2a_rs, hid_ss, hid_rs, ar_ss, ar_rs, pair_ss, pair_rs, back_ss, back_rs,
+    gw_ss, gw_rs, loc_s,
 ):
     groups, head_dim, feats = rf.shape
     toks, width = hid.shape
     half = width // 2
+    parts = half // LANES
+    block = gw_s.shape[2]
+    per = LANES // block
     pairs = groups // 2
     scale = head_dim ** (-0.25)
     norm = feats ** (-0.5)
@@ -72,6 +77,7 @@
     pair = mine // 2
     first = core == 0
     phases = radices(n // groups)
+    partner = flipped(me, 1)
 
     barrier = pltpu.get_barrier_semaphore()
 
@@ -82,6 +88,12 @@
         return carry
 
     lax.fori_loop(1, n, greet, 0)
+    loads = []
+    for i, (src, dst) in enumerate(
+        [(hid_h, hid), (wk_h, wk), (val_h, val), (wq_h, wq), (gout_h, gout), (rf_h, rf)]
+    ):
+        loads.append(pltpu.make_async_copy(src, dst, in_ss.at[i]))
+        loads[-1].start()
 
     def low(shape):
         return lax.broadcasted_iota(jnp.int32, shape, 1) < head_dim
@@ -106,20 +118,61 @@
         got[0] = sent[mine]
         return copies
 
+    for load in loads[:3]:
+        load.wait()
     pack(dot(hid[...], wk[...]) * scale, val[...], kv_s)
     pl.semaphore_wait(barrier, n - 1)
     kv_copies = scatter(0, kv_s, kv_a)
+    for load in loads[3:5]:
+        load.wait()
     pack(dot(hid[...], wq[...]) * scale, gout[...], qg_s)
     qg_copies = scatter(1, qg_s, qg_a)
-    hid_f[0] = hid[:, :half].astype(F32)
-    hid_f[1] = hid[:, half:].astype(F32)
-    hid_copies = []
-    for m in range(1, groups):
+
+    for h in range(2):
+        for q in range(parts):
+            spot = h * half + q * LANES
+            hid_f[h, q] = hid[:, spot : spot + LANES].astype(F32)
+
+    def hidden_copy(q, m):
+        if m & 6 == 6:
+            via, hop = (2, 4) if m == 6 else (5, 2)
+            return remote(
+                hid_r.at[q, via], hid_r.at[q, m], hid_ss.at[q, m], hid_rs.at[q, m], flipped(me, hop)
+            )
         to = flipped(me, m)
-        copy = remote(hid_f.at[to % 2], hid_r.at[m - 1], a2a_ss.at[2, m], a2a_rs.at[2, m], to)
-        copy.start()
-        hid_copies.append(copy)
-
+        return remote(
+            hid_f.at[to % 2, q], hid_r.at[q, m], hid_ss.at[q, m], hid_rs.at[q, m], to
+        )
+
+    relayed = [m for m in range(1, groups) if m & 6 == 6 and m < 8]
+    direct = [m for m in range(1, groups) if m not in relayed]
+    hidden = {(q, m): hidden_copy(q, m) for q in range(parts) for m in range(1, groups)}
+
+    def send_hidden(q):
+        if q < parts:
+            for m in direct:
+                hidden[q, m].start()
+            hid_r[q, 0] = hid_f[core, q]
+
+    ahead = 2
+    for q in range(ahead):
+        send_hidden(q)
+
+    def relay(q):
+        if q >= parts:
+            return
+        for m in relayed:
+            hidden[q, 2 if m == 6 else 5].wait_recv()
+            hidden[q, m].start()
+        send_hidden(q + ahead)
+
+    def hidden_rows(q):
+        for m in range(1, groups):
+            if not (relayed and m in (2, 5)):
+                hidden[q, m].wait_recv()
+        return hid_r[q].reshape(groups * toks, LANES).astype(BF16)
+
+    loads[5].wait()
     rf_high, rf_low = halves(rf[mine])
     rfs[...] = jnp.concatenate([rf_high, rf_high, rf_low, rf_low], axis=0)
     rbs[...] = jnp.concatenate([rf_high, rf_low], axis=0)
@@ -135,7 +188,7 @@
         return ref[2 * c : 2 * c + 2].reshape(2 * toks, ref.shape[2])
 
     def all_reduce(which, total):
-        stride, slot = groups, 0
+        stride = groups
         for f, radix in enumerate(phases):
             ar_s[which, f] = total
             copies = []
@@ -202,6 +255,7 @@
         total = total + dot(turned_high, high) + dot(turned_low, high) + dot(turned_high, rest)
     reduce_q = all_reduce(1, total[lead:])
     next(reduce_q)
+    relay(0)
 
     def feature_grad(x, weighted):
         high, rest = halves(weighted)
@@ -210,6 +264,15 @@
         out = (back - x * jnp.sum(weighted, axis=1, keepdims=True)) * scale
         return jnp.where(low(x.shape), out.astype(BF16).astype(F32), 0.0)
 
+    def pair_copy(which, sent, got, c):
+        two = pl.ds(2 * c, 2)
+        copy = remote(
+            sent.at[two], got.at[two], pair_ss.at[which, c], pair_rs.at[which, c], partner
+        )
+        copy.start()
+        return copy
+
+    pq_copies = []
     for c in range(pairs):
         x = chunk(qg_a, c)
         high, rest = halves(bwd_x[c])
@@ -220,9 +283,7 @@
         placed = jnp.where(first, out, swap(out))
         pq_s[2 * c] = placed[:toks]
         pq_s[2 * c + 1] = placed[toks:]
-    partner = flipped(me, 1)
-    pq_copy = remote(pq_s, pq_r, pair_ss.at[0], pair_rs.at[0], partner)
-    pq_copy.start()
+        pq_copies.append(pair_copy(0, pq_s, pq_r, c))
 
     def give_back(which, sent, got):
         copies = []
@@ -235,13 +296,45 @@
         got[pair] = sent[0]
         return copies
 
-    pq_copy.wait()
-    for m in range(groups):
-        dq_p[m] = pq_s[m] + pq_r[m ^ 1]
-    dq_copies = give_back(0, dq_p, dq_a)
+    relay(1)
+    for c in range(pairs):
+        pq_copies[c].wait()
+        for m in (2 * c, 2 * c + 1):
+            both = pq_s[m] + pq_r[m ^ 1]
+            dq_p[m] = both
+            turned[0, :, m * toks : (m + 1) * toks] = both.T.astype(BF16)
+
+    def weight_part(which, q, rows):
+        total = dot(turned[which], rows).T
+        gw_s[which, q * per : (q + 1) * per] = total.reshape(per, block, LANES)
+
+    def weight_sends(which, q):
+        def start(i, carry):
+            to = core * (n // 2) + i
+
+            @pl.when(to != me)
+            def _():
+                remote(
+                    gw_s.at[which, i], gw_r.at[which, me // 2],
+                    gw_ss.at[which, i], gw_rs.at[which, me // 2], to,
+                ).start()
+
+            @pl.when(to == me)
+            def _():
+                pltpu.make_async_copy(
+                    gw_s.at[which, i], gw_r.at[which, me // 2], loc_s.at[which]
+                ).start()
+
+            return carry
+
+        lax.fori_loop(q * per, (q + 1) * per, start, 0)
+
+    weight_part(0, 0, hidden_rows(0))
 
     gs_high, gs_low = finish(reduce_q)
+    weight_sends(0, 0)
     gs_both = jnp.concatenate([gs_high, gs_low], axis=0)
+    pk_copies = []
     for c in range(pairs):
         x = chunk(kv_a, c)
         mask = low(x.shape)
@@ -256,117 +349,118 @@
         packed = jnp.where(mask, out, gv)
         pk_s[2 * c] = packed[:toks]
         pk_s[2 * c + 1] = packed[toks:]
-    pk_copy = remote(pk_s, pk_r, pair_ss.at[1], pair_rs.at[1], partner)
-    pk_copy.start()
-
-    for copy in hid_copies:
+        pk_copies.append(pair_copy(1, pk_s, pk_r, c))
+    relay(2)
+    weight_part(0, 1, hidden_rows(1))
+    weight_sends(0, 1)
+    for c in range(pairs):
+        pk_copies[c].wait()
+        for m in (2 * c, 2 * c + 1):
+            own, theirs = pk_s[m], pk_r[m ^ 1]
+            one = jnp.where(first, own, theirs)
+            two = jnp.where(first, theirs, own)
+            mask = low(own.shape)
+            both = jnp.where(mask, one, swap(two))
+            dk_p[m] = both
+            turned[1, :, m * toks : (m + 1) * toks] = both.T.astype(BF16)
+            gv_p[m] = jnp.where(mask, swap(one), two)
+    for q in range(2):
+        weight_part(1, q, hid_r[q].reshape(groups * toks, LANES).astype(BF16))
+        weight_sends(1, q)
+    for q in range(2, parts):
+        relay(q + 1)
+        if q == parts - 1:
+            dq_copies = give_back(0, dq_p, dq_a)
+            dk_copies = give_back(1, dk_p, dk_a)
+        rows = hidden_rows(q)
+        for which in range(2):
+            weight_part(which, q, rows)
+            weight_sends(which, q)
+    gv_copies = give_back(2, gv_p, gv_a)
+
+    def joined(ref):
+        return jnp.concatenate([ref[p] for p in range(pairs)], axis=1).astype(BF16)
+
+    for copy in dq_copies:
         copy.wait()
+    o_hid[...] = dot_t(joined(dq_a), wq[...])
+    for copy in dk_copies:
+        copy.wait()
+    o_hid[...] += dot_t(joined(dk_a), wk[...])
+    for copy in gv_copies:
+        copy.wait()
+    o_val[...] = joined(gv_a)
 
     owner_half = me // (n // 2)
 
-    def weight_sends(which, grads_p):
-        total = jnp.zeros((LANES, half), F32)
-        for m in range(groups):
-            rows = hid_f[core] if m == 0 else hid_r[m - 1]
-            total = total + dot(grads_p[m].T.astype(BF16), rows.astype(BF16))
-        gw_s[which] = total.T.reshape(gw_s.shape[1:])
-
-        def start(i, carry):
-            to = core * (n // 2) + i
-
-            @pl.when(to != me)
-            def _():
-                remote(
-                    gw_s.at[which, i], gw_r.at[which, me // 2],
-                    gw_ss.at[which, i], gw_rs.at[which, me // 2], to,
-                ).start()
-
-            @pl.when(to == me)
-            def _():
-                pltpu.make_async_copy(
-                    gw_s.at[which, i], gw_r.at[which, me // 2], loc_s.at[which]
-                ).start()
-
-            return carry
-
-        lax.fori_loop(0, n // 2, start, 0)
-
-    def weight_waits(which, out):
-        def wait(i, carry):
-            to = core * (n // 2) + i
-            source = 2 * i + owner_half
-            here = remote(
-                gw_s.at[which, i], gw_r.at[which, i], gw_ss.at[which, i], gw_rs.at[which, i], partner
-            )
-
-            @pl.when(to != me)
-            def _():
-                here.wait_send()
-
-            @pl.when(to == me)
-            def _():
-                pltpu.make_async_copy(
-                    gw_s.at[which, i], gw_r.at[which, me // 2], loc_s.at[which]
-                ).wait()
-
-            @pl.when(source != me)
-            def _():
-                here.wait_recv()
-
-            return carry
-
-        lax.fori_loop(0, n // 2, wait, 0)
+    def weight_wait(which, i):
+        to = core * (n // 2) + i
+        source = 2 * i + owner_half
+        here = remote(
+            gw_s.at[which, i], gw_r.at[which, i], gw_ss.at[which, i], gw_rs.at[which, i], partner
+        )
+
+        @pl.when(to != me)
+        def _():
+            here.wait_send()
+
+        @pl.when(to == me)
+        def _():
+            pltpu.make_async_copy(
+                gw_s.at[which, i], gw_r.at[which, me // 2], loc_s.at[which]
+            ).wait()
+
+        @pl.when(source != me)
+        def _():
+            here.wait_recv()
+
+    def wait_both(i, carry):
+        weight_wait(0, i)
+        weight_wait(1, i)
+        return carry
+
+    lax.fori_loop(0, n // 2, wait_both, 0)
+    for which, out in ((0, o_gq), (1, o_gk)):
         for p in range(pairs):
             total = gw_r[which, p]
             for i in range(p + pairs, n // 2, pairs):
                 total = total + gw_r[which, i]
             out[:, p * LANES : (p + 1) * LANES] = total
-
-    weight_sends(0, dq_p)
-
-    pk_copy.wait()
-    for m in range(groups):
-        own, theirs = pk_s[m], pk_r[m ^ 1]
-        one = jnp.where(first, own, theirs)
-        two = jnp.where(first, theirs, own)
-        mask = low(own.shape)
-        dk_p[m] = jnp.where(mask, one, swap(two))
-        gv_p[m] = jnp.where(mask, swap(one), two)
-    weight_sends(1, dk_p)
-    dk_copies = give_back(1, dk_p, dk_a)
-    gv_copies = give_back(2, gv_p, gv_a)
-
-    def joined(ref):
-        return jnp.concatenate([ref[p] for p in range(pairs)], axis=1).astype(BF16)
-
-    for copy in dq_copies:
+    for copy in hidden.values():
+        copy.wait_send()
+
+
+def store(*refs):
+    count = len(refs) // 2
+    sems = refs[-1]
+    copies = [
+        pltpu.make_async_copy(refs[i], refs[count + i], sems.at[i]) for i in range(count)
+    ]
+    for copy in copies:
+        copy.start()
+    for copy in copies:
         copy.wait()
-    for copy in dk_copies:
-        copy.wait()
-    o_hid[...] = dot_t(joined(dq_a), wq[...]) + dot_t(joined(dk_a), wk[...])
-    for copy in gv_copies:
-        copy.wait()
-    o_val[...] = joined(gv_a)
-    weight_waits(0, o_gq)
-    weight_waits(1, o_gk)
-
-
-def shards(n, hidden, query_weight, key_weight, values, grad_out, random_feats):
+
+
+def shards(n, *args):
+    hidden, random_feats = args[0], args[5]
     toks, width = hidden.shape
     groups, head_dim, feats = random_feats.shape
     cols = groups * head_dim
     pairs = groups // 2
     block = width // n
+    parts = width // 2 // LANES
     phases = len(radices(n // groups))
     rows = head_dim + 8
     tok_block = (groups, toks, LANES)
-    scratch = [
-        pltpu.VMEM((2, toks, width // 2), F32),
-        pltpu.VMEM((groups - 1, toks, width // 2), F32),
-        pltpu.VMEM(tok_block, F32),
-        pltpu.VMEM(tok_block, F32),
-        pltpu.VMEM(tok_block, F32),
-        pltpu.VMEM(tok_block, F32),
+    own_block = (pairs, toks, LANES)
+    scratch = [pltpu.VMEM(a.shape, a.dtype) for a in args]
+    scratch += [
+        pltpu.VMEM((2, parts, toks, LANES), F32),
+        pltpu.VMEM((parts,) + tok_block, F32),
+    ]
+    scratch += [pltpu.VMEM(tok_block, F32)] * 4
+    scratch += [
         pltpu.VMEM((4 * head_dim, feats), BF16),
         pltpu.VMEM((2 * head_dim, feats), BF16),
         pltpu.VMEM((pairs, 2 * toks, feats), F32),
@@ -374,47 +468,46 @@
         pltpu.VMEM((pairs, 2 * toks, LANES), F32),
         pltpu.VMEM((2, phases, rows, feats), F32),
         pltpu.VMEM((2, phases, 3, rows, feats), F32),
-        pltpu.VMEM(tok_block, F32),
-        pltpu.VMEM(tok_block, F32),
-        pltpu.VMEM(tok_block, F32),
-        pltpu.VMEM(tok_block, F32),
-        pltpu.VMEM(tok_block, F32),
-        pltpu.VMEM(tok_block, F32),
-        pltpu.VMEM(tok_block, F32),
-        pltpu.VMEM((pairs, toks, LANES), F32),
-        pltpu.VMEM((pairs, toks, LANES), F32),
-        pltpu.VMEM((pairs, toks, LANES), F32),
-        pltpu.VMEM((2, n // 2, block, LANES), F32),
-        pltpu.VMEM((2, n // 2, block, LANES), F32),
-        pltpu.SemaphoreType.DMA((3, groups)),
-        pltpu.SemaphoreType.DMA((3, groups)),
-        pltpu.SemaphoreType.DMA((2, phases, 4)),
-        pltpu.SemaphoreType.DMA((2, phases, 4)),
-        pltpu.SemaphoreType.DMA((2,)),
-        pltpu.SemaphoreType.DMA((2,)),
-        pltpu.SemaphoreType.DMA((3, groups)),
-        pltpu.SemaphoreType.DMA((3, groups)),
-        pltpu.SemaphoreType.DMA((2, n // 2)),
-        pltpu.SemaphoreType.DMA((2, n // 2)),
-        pltpu.SemaphoreType.DMA((2,)),
     ]
+    scratch += [pltpu.VMEM(tok_block, F32)] * 7
+    scratch += [pltpu.VMEM((2, LANES, groups * toks), BF16)]
+    scratch += [pltpu.VMEM(own_block, F32)] * 3
+    scratch += [pltpu.VMEM((2, n // 2, block, LANES), F32)] * 2
+    scratch += [pltpu.SemaphoreType.DMA((6,))]
+    scratch += [pltpu.SemaphoreType.DMA((2, groups))] * 2
+    scratch += [pltpu.SemaphoreType.DMA((parts, groups))] * 2
+    scratch += [pltpu.SemaphoreType.DMA((2, phases, 4))] * 2
+    scratch += [pltpu.SemaphoreType.DMA((2, pairs))] * 2
+    scratch += [pltpu.SemaphoreType.DMA((3, groups))] * 2
+    scratch += [pltpu.SemaphoreType.DMA((2, n // 2))] * 2
+    scratch += [pltpu.SemaphoreType.DMA((2,))]
     vmem = pl.BlockSpec(memory_space=pltpu.VMEM)
-    return pl.pallas_call(
+    anywhere = pl.BlockSpec(memory_space=pl.ANY)
+    shapes = (
+        jax.ShapeDtypeStruct((toks, width), F32),
+        jax.ShapeDtypeStruct((toks, cols), BF16),
+        jax.ShapeDtypeStruct((block, cols), F32),
+        jax.ShapeDtypeStruct((block, cols), F32),
+    )
+    out = pl.pallas_call(
         functools.partial(kernel, n),
-        out_shape=(
-            jax.ShapeDtypeStruct((toks, width), F32),
-            jax.ShapeDtypeStruct((toks, cols), BF16),
-            jax.ShapeDtypeStruct((block, cols), F32),
-            jax.ShapeDtypeStruct((block, cols), F32),
-        ),
-        in_specs=[vmem] * 6,
+        out_shape=tuple(pltpu.VMEM(a.shape, a.dtype) for a in shapes),
+        in_specs=[anywhere] * 6,
         out_specs=(vmem,) * 4,
         scratch_shapes=scratch,
         compiler_params=pltpu.CompilerParams(
             collective_id=0, has_side_effects=True, vmem_limit_bytes=56 * 2**20
         ),
         name="backward",
-    )(hidden, query_weight, key_weight, values, grad_out, random_feats)
+    )(*args)
+    return pl.pallas_call(
+        store,
+        out_shape=shapes,
+        in_specs=[vmem] * 4,
+        out_specs=(anywhere,) * 4,
+        scratch_shapes=[pltpu.SemaphoreType.DMA((4,))],
+        name="store",
+    )(*[pltpu.with_memory_space_constraint(a, pltpu.VMEM) for a in out])
 
 
 def solution(mesh):

time: 67.5 us -> 57.8 us (0.86)
  Pallas kernels: 62.3 us -> 56.3 us
  local copies, waits for them, and re-layouts: 4.28 us -> 0 us
    pallas_call x1 -> x2, Pallas kernels: 62.3 us -> 56.3 us  [the longest x1 55.4 us: shards(): pl.pallas_call(functools.partial(kernel, n), out_shape=tuple((pltpu.VMEM(...]
    unnamed x10 -> x0, local copies, waits for them, and re-layouts: 4.28 us -> none
where the time goes in v2:
time: 57.8 us; the launch traced here: 56.9 us
  Pallas kernels  56.3 us (97%)
  between operations  0.64 us (1%)
    pallas_call x1, Pallas kernels, shards(): pl.pallas_call(functools.partial(kernel, n), out_shape=tuple((pltpu.VMEM(...  55.4 us

profile of v2, /device:TPU:0, one launch (start us, length us, event | category | flops | bytes accessed | tf_op | source)
XLA Modules:
  0.0 56.9 jit_solution(6199653201502669483)
XLA Ops:
  0.6 55.4 %backward.1 = (f32[128,1024]{1,0:T(8,128)S(1)}, bf16[128,512]{1,0:T(8,128)(2,1)S(1)}, f32[32,512]{1,0:T(8,128)S(1)}, f32[32,512]{1,0:T(8,128)S(1)}) custom-call(bf16[128,1024]{1,0:T(8,128)(2,1)} %hid_h.1, bf16[1024,512]{1,0:T(8,128)(2,1)} %wq_h.1, bf16[1024,512]{1,0:T(8,128)(2,1)} %wk_h.1, bf16[128,512]{1,0:T(8,128)(2,1)} %val_h.1, bf16[128,512]{1,0:T(8,128)(2,1)} %gout_h.1, ...), custom_call_target="tpu_custom_call" | custom-call | tf_op jit(solution)/shard_map/backward/pallas_call | solution.py:492
  56.0 0.9 %store.1 = (f32[128,1024]{1,0:T(8,128)}, bf16[128,512]{1,0:T(8,128)(2,1)}, f32[32,512]{1,0:T(8,128)}, f32[32,512]{1,0:T(8,128)}) custom-call(f32[128,1024]{1,0:T(8,128)S(1)} %get-tuple-element.8.refs_0_, bf16[128,512]{1,0:T(8,128)(2,1)S(1)} %get-tuple-element.9.refs_1_, f32[32,512]{1,0:T(8,128)S(1)} %get-tuple-element.10.refs_2_, ...), custom_call_target="tpu_custom_call" | custom-call | tf_op jit(solution)/shard_map/store/pallas_call | solution.py:503

commit v3 on v2

--- a/solution.py
+++ b/solution.py
@@ -47,6 +47,10 @@
     return pltpu.roll(x, LANES // 2, 1)
 
 
+def settle(ref, sem):
+    pltpu.make_async_copy(ref, ref, sem).wait()
+
+
 def remote(src, dst, send_sem, recv_sem, peer):
     return pltpu.make_async_remote_copy(
         src_ref=src, dst_ref=dst, send_sem=send_sem, recv_sem=recv_sem,
@@ -60,7 +64,7 @@
     hid_f, hid_r, kv_s, kv_a, qg_s, qg_a, rfs, rbs, feat_k, feat_q, bwd_x,
     ar_s, ar_r, pq_s, pq_r, pk_s, pk_r, dq_p, dk_p, gv_p, turned, dq_a, dk_a, gv_a, gw_s, gw_r,
     in_ss, a2a_ss, a2a_rs, hid_ss, hid_rs, ar_ss, ar_rs, pair_ss, pair_rs, back_ss, back_rs,
-    gw_ss, gw_rs, loc_s,
+    gw_ss, gw_rs,
 ):
     groups, head_dim, feats = rf.shape
     toks, width = hid.shape
@@ -107,69 +111,66 @@
             out[2 * p + 1] = jnp.where(mask, swap(a), b)
 
     def scatter(which, sent, got):
-        copies = []
         for m in range(1, groups):
             to = flipped(me, m)
-            copy = remote(
-                sent.at[to % groups], got.at[m], a2a_ss.at[which, m], a2a_rs.at[which, m], to
-            )
-            copy.start()
-            copies.append(copy)
+            remote(
+                sent.at[to % groups], got.at[m], a2a_ss.at[which], a2a_rs.at[which, m // 2], to
+            ).start()
         got[0] = sent[mine]
-        return copies
+
+    def scattered(which, got, c):
+        skip = 1 if c == 0 else 0
+        settle(got.at[pl.ds(2 * c + skip, 2 - skip)], a2a_rs.at[which, c])
 
     for load in loads[:3]:
         load.wait()
     pack(dot(hid[...], wk[...]) * scale, val[...], kv_s)
     pl.semaphore_wait(barrier, n - 1)
-    kv_copies = scatter(0, kv_s, kv_a)
+    scatter(0, kv_s, kv_a)
     for load in loads[3:5]:
         load.wait()
     pack(dot(hid[...], wq[...]) * scale, gout[...], qg_s)
-    qg_copies = scatter(1, qg_s, qg_a)
+    scatter(1, qg_s, qg_a)
 
     for h in range(2):
         for q in range(parts):
             spot = h * half + q * LANES
             hid_f[h, q] = hid[:, spot : spot + LANES].astype(F32)
 
-    def hidden_copy(q, m):
-        if m & 6 == 6:
-            via, hop = (2, 4) if m == 6 else (5, 2)
-            return remote(
-                hid_r.at[q, via], hid_r.at[q, m], hid_ss.at[q, m], hid_rs.at[q, m], flipped(me, hop)
-            )
-        to = flipped(me, m)
-        return remote(
-            hid_f.at[to % 2, q], hid_r.at[q, m], hid_ss.at[q, m], hid_rs.at[q, m], to
-        )
-
     relayed = [m for m in range(1, groups) if m & 6 == 6 and m < 8]
     direct = [m for m in range(1, groups) if m not in relayed]
-    hidden = {(q, m): hidden_copy(q, m) for q in range(parts) for m in range(1, groups)}
+    passed_on = [2, 5] if relayed else []
+    ahead = 3
+
+    def hidden_start(q, m):
+        if m in relayed:
+            via, hop = (2, 4) if m == 6 else (5, 2)
+            source, to = hid_r.at[q, via], flipped(me, hop)
+        else:
+            to = flipped(me, m)
+            source = hid_f.at[to % 2, q]
+        recv = hid_rs.at[q, 1 if m in passed_on else 0]
+        remote(source, hid_r.at[q, m], hid_ss.at[0], recv, to).start()
 
     def send_hidden(q):
         if q < parts:
-            for m in direct:
-                hidden[q, m].start()
+            for m in passed_on + [m for m in direct if m not in passed_on]:
+                hidden_start(q, m)
             hid_r[q, 0] = hid_f[core, q]
 
-    ahead = 2
     for q in range(ahead):
         send_hidden(q)
 
     def relay(q):
-        if q >= parts:
-            return
-        for m in relayed:
-            hidden[q, 2 if m == 6 else 5].wait_recv()
-            hidden[q, m].start()
-        send_hidden(q + ahead)
+        if q < parts:
+            if passed_on:
+                settle(hid_r.at[q, pl.ds(0, len(passed_on))], hid_rs.at[q, 1])
+            for m in relayed:
+                hidden_start(q, m)
+            send_hidden(q + ahead)
 
     def hidden_rows(q):
-        for m in range(1, groups):
-            if not (relayed and m in (2, 5)):
-                hidden[q, m].wait_recv()
+        settle(hid_r.at[q, pl.ds(0, groups - 1 - len(passed_on))], hid_rs.at[q, 0])
         return hid_r[q].reshape(groups * toks, LANES).astype(BF16)
 
     loads[5].wait()
@@ -191,17 +192,16 @@
         stride = groups
         for f, radix in enumerate(phases):
             ar_s[which, f] = total
-            copies = []
             for d in range(1, radix):
-                copy = remote(
+                remote(
                     ar_s.at[which, f], ar_r.at[which, f, d - 1],
-                    ar_ss.at[which, f, d], ar_rs.at[which, f, d], flipped(me, d, stride),
-                )
-                copy.start()
-                copies.append(copy)
+                    ar_ss.at[which, f], ar_rs.at[which, f], flipped(me, d, stride),
+                ).start()
             yield
-            for d, copy in enumerate(copies):
-                copy.wait()
+            came = ar_r.at[which, f, pl.ds(0, radix - 1)]
+            settle(came, ar_rs.at[which, f])
+            settle(came, ar_ss.at[which, f])
+            for d in range(radix - 1):
                 total = total + ar_r[which, f, d]
             stride *= radix
         summed = jnp.concatenate(
@@ -218,9 +218,7 @@
 
     total = jnp.zeros((LANES, feats), F32)
     for c in range(pairs):
-        for m in (2 * c, 2 * c + 1):
-            if m > 0:
-                kv_copies[m - 1].wait()
+        scattered(0, kv_a, c)
         x = chunk(kv_a, c)
         b = features(x)
         feat_k[c] = b
@@ -231,9 +229,7 @@
     next(reduce_k)
 
     for c in range(pairs):
-        for m in (2 * c, 2 * c + 1):
-            if m > 0:
-                qg_copies[m - 1].wait()
+        scattered(1, qg_a, c)
         feat_q[c] = features(chunk(qg_a, c))
 
     st_high, st_low = finish(reduce_k)
@@ -266,13 +262,13 @@
 
     def pair_copy(which, sent, got, c):
         two = pl.ds(2 * c, 2)
-        copy = remote(
-            sent.at[two], got.at[two], pair_ss.at[which, c], pair_rs.at[which, c], partner
-        )
-        copy.start()
-        return copy
-
-    pq_copies = []
+        remote(
+            sent.at[two], got.at[two], pair_ss.at[which], pair_rs.at[which, c], partner
+        ).start()
+
+    def paired(which, got, c):
+        settle(got.at[pl.ds(2 * c, 2)], pair_rs.at[which, c])
+
     for c in range(pairs):
         x = chunk(qg_a, c)
         high, rest = halves(bwd_x[c])
@@ -283,22 +279,21 @@
         placed = jnp.where(first, out, swap(out))
         pq_s[2 * c] = placed[:toks]
         pq_s[2 * c + 1] = placed[toks:]
-        pq_copies.append(pair_copy(0, pq_s, pq_r, c))
+        pair_copy(0, pq_s, pq_r, c)
 
     def give_back(which, sent, got):
-        copies = []
         for m in range(2, groups, 2):
-            copy = remote(
-                sent.at[m], got.at[pair], back_ss.at[which, m], back_rs.at[which, m], flipped(me, m)
-            )
-            copy.start()
-            copies.append(copy)
+            remote(
+                sent.at[m], got.at[pair], back_ss.at[which], back_rs.at[which], flipped(me, m)
+            ).start()
         got[pair] = sent[0]
-        return copies
+
+    def given_back(which, got):
+        settle(got.at[pl.ds(0, pairs - 1)], back_rs.at[which])
 
     relay(1)
     for c in range(pairs):
-        pq_copies[c].wait()
+        paired(0, pq_r, c)
         for m in (2 * c, 2 * c + 1):
             both = pq_s[m] + pq_r[m ^ 1]
             dq_p[m] = both
@@ -316,25 +311,25 @@
             def _():
                 remote(
                     gw_s.at[which, i], gw_r.at[which, me // 2],
-                    gw_ss.at[which, i], gw_rs.at[which, me // 2], to,
+                    gw_ss.at[which], gw_rs.at[which], to,
                 ).start()
 
             @pl.when(to == me)
             def _():
                 pltpu.make_async_copy(
-                    gw_s.at[which, i], gw_r.at[which, me // 2], loc_s.at[which]
+                    gw_s.at[which, i], gw_r.at[which, me // 2], gw_rs.at[which]
                 ).start()
 
             return carry
 
         lax.fori_loop(q * per, (q + 1) * per, start, 0)
 
+    relay(2)
     weight_part(0, 0, hidden_rows(0))
 
     gs_high, gs_low = finish(reduce_q)
     weight_sends(0, 0)
     gs_both = jnp.concatenate([gs_high, gs_low], axis=0)
-    pk_copies = []
     for c in range(pairs):
         x = chunk(kv_a, c)
         mask = low(x.shape)
@@ -349,12 +344,13 @@
         packed = jnp.where(mask, out, gv)
         pk_s[2 * c] = packed[:toks]
         pk_s[2 * c + 1] = packed[toks:]
-        pk_copies.append(pair_copy(1, pk_s, pk_r, c))
-    relay(2)
+        pair_copy(1, pk_s, pk_r, c)
+        if c == pairs // 2 - 1:
+            relay(3)
     weight_part(0, 1, hidden_rows(1))
     weight_sends(0, 1)
     for c in range(pairs):
-        pk_copies[c].wait()
+        paired(1, pk_r, c)
         for m in (2 * c, 2 * c + 1):
             own, theirs = pk_s[m], pk_r[m ^ 1]
             one = jnp.where(first, own, theirs)
@@ -367,67 +363,52 @@
     for q in range(2):
         weight_part(1, q, hid_r[q].reshape(groups * toks, LANES).astype(BF16))
         weight_sends(1, q)
+    give_back(0, dq_p, dq_a)
+    give_back(1, dk_p, dk_a)
     for q in range(2, parts):
-        relay(q + 1)
-        if q == parts - 1:
-            dq_copies = give_back(0, dq_p, dq_a)
-            dk_copies = give_back(1, dk_p, dk_a)
+        if q > 2:
+            relay(q + 1)
         rows = hidden_rows(q)
         for which in range(2):
             weight_part(which, q, rows)
             weight_sends(which, q)
-    gv_copies = give_back(2, gv_p, gv_a)
+    give_back(2, gv_p, gv_a)
 
     def joined(ref):
         return jnp.concatenate([ref[p] for p in range(pairs)], axis=1).astype(BF16)
 
-    for copy in dq_copies:
-        copy.wait()
+    given_back(0, dq_a)
     o_hid[...] = dot_t(joined(dq_a), wq[...])
-    for copy in dk_copies:
-        copy.wait()
+    given_back(1, dk_a)
     o_hid[...] += dot_t(joined(dk_a), wk[...])
-    for copy in gv_copies:
-        copy.wait()
+    given_back(2, gv_a)
     o_val[...] = joined(gv_a)
 
-    owner_half = me // (n // 2)
-
-    def weight_wait(which, i):
-        to = core * (n // 2) + i
-        source = 2 * i + owner_half
-        here = remote(
-            gw_s.at[which, i], gw_r.at[which, i], gw_ss.at[which, i], gw_rs.at[which, i], partner
-        )
-
-        @pl.when(to != me)
-        def _():
-            here.wait_send()
-
-        @pl.when(to == me)
-        def _():
-            pltpu.make_async_copy(
-                gw_s.at[which, i], gw_r.at[which, me // 2], loc_s.at[which]
-            ).wait()
-
-        @pl.when(source != me)
-        def _():
-            here.wait_recv()
-
-    def wait_both(i, carry):
-        weight_wait(0, i)
-        weight_wait(1, i)
-        return carry
-
-    lax.fori_loop(0, n // 2, wait_both, 0)
+    for which in range(2):
+        settle(gw_r.at[which], gw_rs.at[which])
     for which, out in ((0, o_gq), (1, o_gk)):
         for p in range(pairs):
             total = gw_r[which, p]
             for i in range(p + pairs, n // 2, pairs):
                 total = total + gw_r[which, i]
             out[:, p * LANES : (p + 1) * LANES] = total
-    for copy in hidden.values():
-        copy.wait_send()
+    for which in range(2):
+        others = kv_a.at[pl.ds(1, groups - 1)]
+        settle(others, a2a_ss.at[which])
+        settle(pk_s, pair_ss.at[which])
+        own_set = me // (n // 2) == core
+
+        @pl.when(own_set)
+        def _():
+            settle(gw_s.at[which, pl.ds(0, n // 2 - 1)], gw_ss.at[which])
+
+        @pl.when(jnp.logical_not(own_set))
+        def _():
+            settle(gw_s.at[which], gw_ss.at[which])
+
+    for which in range(3):
+        settle(dq_a.at[pl.ds(0, pairs - 1)], back_ss.at[which])
+    settle(hid_r.at[:, pl.ds(1, groups - 1)], hid_ss.at[0])
 
 
 def store(*refs):
@@ -473,14 +454,11 @@
     scratch += [pltpu.VMEM((2, LANES, groups * toks), BF16)]
     scratch += [pltpu.VMEM(own_block, F32)] * 3
     scratch += [pltpu.VMEM((2, n // 2, block, LANES), F32)] * 2
-    scratch += [pltpu.SemaphoreType.DMA((6,))]
-    scratch += [pltpu.SemaphoreType.DMA((2, groups))] * 2
-    scratch += [pltpu.SemaphoreType.DMA((parts, groups))] * 2
-    scratch += [pltpu.SemaphoreType.DMA((2, phases, 4))] * 2
-    scratch += [pltpu.SemaphoreType.DMA((2, pairs))] * 2
-    scratch += [pltpu.SemaphoreType.DMA((3, groups))] * 2
-    scratch += [pltpu.SemaphoreType.DMA((2, n // 2))] * 2
-    scratch += [pltpu.SemaphoreType.DMA((2,))]
+    for shape in (
+        (6,), (2,), (2, pairs), (1,), (parts, 2), (2, phases), (2, phases), (2,), (2, pairs),
+        (3,), (3,), (2,), (2,),
+    ):
+        scratch.append(pltpu.SemaphoreType.DMA(shape))
     vmem = pl.BlockSpec(memory_space=pltpu.VMEM)
     anywhere = pl.BlockSpec(memory_space=pl.ANY)
     shapes = (

time: 57.8 us -> 54.7 us (0.946)
  the two profiles are of different devices: /device:TPU:0 before, /device:TPU:8 now
where the time goes in v3:
time: 54.7 us; the launch traced here: 54.5 us
  Pallas kernels  53.9 us (99%)
  between operations  0.64 us (1%)
    pallas_call x1, Pallas kernels, shards(): pl.pallas_call(functools.partial(kernel, n), out_shape=tuple((pltpu.VMEM(...  53 us

profile of v3, /device:TPU:8, one launch (start us, length us, event | category | flops | bytes accessed | tf_op | source)
XLA Modules:
  0.0 54.5 jit_solution(4200398414706330402)
XLA Ops:
  0.6 53.0 %backward.1 = (f32[128,1024]{1,0:T(8,128)S(1)}, bf16[128,512]{1,0:T(8,128)(2,1)S(1)}, f32[32,512]{1,0:T(8,128)S(1)}, f32[32,512]{1,0:T(8,128)S(1)}) custom-call(bf16[128,1024]{1,0:T(8,128)(2,1)} %hid_h.1, bf16[1024,512]{1,0:T(8,128)(2,1)} %wq_h.1, bf16[1024,512]{1,0:T(8,128)(2,1)} %wk_h.1, bf16[128,512]{1,0:T(8,128)(2,1)} %val_h.1, bf16[128,512]{1,0:T(8,128)(2,1)} %gout_h.1, ...), custom_call_target="tpu_custom_call" | custom-call | tf_op jit(solution)/shard_map/backward/pallas_call | solution.py:470
  53.6 0.9 %store.1 = (f32[128,1024]{1,0:T(8,128)}, bf16[128,512]{1,0:T(8,128)(2,1)}, f32[32,512]{1,0:T(8,128)}, f32[32,512]{1,0:T(8,128)}) custom-call(f32[128,1024]{1,0:T(8,128)S(1)} %get-tuple-element.8.refs_0_, bf16[128,512]{1,0:T(8,128)(2,1)S(1)} %get-tuple-element.9.refs_1_, f32[32,512]{1,0:T(8,128)S(1)} %get-tuple-element.10.refs_2_, ...), custom_call_target="tpu_custom_call" | custom-call | tf_op jit(solution)/shard_map/store/pallas_call | solution.py:481

commit v4 on v3

--- a/solution.py
+++ b/solution.py
@@ -62,9 +62,9 @@
     n, hid_h, wq_h, wk_h, val_h, gout_h, rf_h, o_hid, o_val, o_gq, o_gk,
     hid, wq, wk, val, gout, rf,
     hid_f, hid_r, kv_s, kv_a, qg_s, qg_a, rfs, rbs, feat_k, feat_q, bwd_x,
-    ar_s, ar_r, pq_s, pq_r, pk_s, pk_r, dq_p, dk_p, gv_p, turned, dq_a, dk_a, gv_a, gw_s, gw_r,
+    ar_s, ar_r, pair_s, pair_r, dq_p, turned, feat_l, states, dq_a, gw_s, gw_r,
     in_ss, a2a_ss, a2a_rs, hid_ss, hid_rs, ar_ss, ar_rs, pair_ss, pair_rs, back_ss, back_rs,
-    gw_ss, gw_rs,
+    st_ss, st_rs, gw_ss, gw_rs,
 ):
     groups, head_dim, feats = rf.shape
     toks, width = hid.shape
@@ -174,15 +174,16 @@
         return hid_r[q].reshape(groups * toks, LANES).astype(BF16)
 
     loads[5].wait()
-    rf_high, rf_low = halves(rf[mine])
-    rfs[...] = jnp.concatenate([rf_high, rf_high, rf_low, rf_low], axis=0)
-    rbs[...] = jnp.concatenate([rf_high, rf_low], axis=0)
-
-    def features(x):
+    for j in range(groups):
+        rf_high, rf_low = halves(rf[j])
+        rfs[j] = jnp.concatenate([rf_high, rf_high, rf_low, rf_low], axis=0)
+        rbs[j] = jnp.concatenate([rf_high, rf_low], axis=0)
+
+    def features(x, j):
         rows = jnp.where(low(x.shape), x, 0.0)
         high = rows.astype(BF16).astype(F32)
         both = (high + swap(rows - high)).astype(BF16)
-        logits = dot(jnp.concatenate([both, both], axis=1), rfs[...])
+        logits = dot(jnp.concatenate([both, both], axis=1), rfs[j])
         return jnp.exp(logits - 0.5 * jnp.sum(rows * rows, axis=1, keepdims=True)) * norm
 
     def chunk(ref, c):
@@ -204,23 +205,30 @@
             for d in range(radix - 1):
                 total = total + ar_r[which, f, d]
             stride *= radix
-        summed = jnp.concatenate(
-            [jnp.broadcast_to(total[7:8], (head_dim, feats)), total[8:]], axis=0
-        )
-        yield halves(summed)
+        yield total
 
     def finish(steps):
         for got in steps:
             if got is not None:
                 return got
 
+    def spread(total):
+        return halves(
+            jnp.concatenate(
+                [jnp.broadcast_to(total[7:8], (head_dim, feats)), total[8:]], axis=0
+            )
+        )
+
     lead = head_dim - 8
+
+    for j in range(groups):
+        feat_l[j] = features(kv_s[j], j)
 
     total = jnp.zeros((LANES, feats), F32)
     for c in range(pairs):
         scattered(0, kv_a, c)
         x = chunk(kv_a, c)
-        b = features(x)
+        b = features(x, mine)
         feat_k[c] = b
         high, rest = halves(b)
         ones = jnp.where(low(x.shape), 1.0, x).T.astype(BF16)
@@ -230,9 +238,9 @@
 
     for c in range(pairs):
         scattered(1, qg_a, c)
-        feat_q[c] = features(chunk(qg_a, c))
-
-    st_high, st_low = finish(reduce_k)
+        feat_q[c] = features(chunk(qg_a, c), mine)
+
+    st_high, st_low = spread(finish(reduce_k))
     st_both = jnp.concatenate([st_high, st_low], axis=0)
     total = jnp.zeros((LANES, feats), F32)
     for c in range(pairs):
@@ -253,21 +261,30 @@
     next(reduce_q)
     relay(0)
 
-    def feature_grad(x, weighted):
+    def feature_grad(x, weighted, j):
         high, rest = halves(weighted)
-        back = dot_t(high, rbs[...]) + dot_t(rest, rbs[...])
+        back = dot_t(high, rbs[j]) + dot_t(rest, rbs[j])
         back = back + swap(back)
         out = (back - x * jnp.sum(weighted, axis=1, keepdims=True)) * scale
         return jnp.where(low(x.shape), out.astype(BF16).astype(F32), 0.0)
 
-    def pair_copy(which, sent, got, c):
+    def pair_send(which, c, out):
+        placed = jnp.where(first, out, swap(out))
+        pair_s[which, 2 * c] = placed[:toks]
+        pair_s[which, 2 * c + 1] = placed[toks:]
         two = pl.ds(2 * c, 2)
         remote(
-            sent.at[two], got.at[two], pair_ss.at[which], pair_rs.at[which, c], partner
+            pair_s.at[which, two], pair_r.at[which, two],
+            pair_ss.at[which], pair_rs.at[which, c], partner,
         ).start()
 
-    def paired(which, got, c):
-        settle(got.at[pl.ds(2 * c, 2)], pair_rs.at[which, c])
+    def paired(which, c):
+        settle(pair_r.at[which, pl.ds(2 * c, 2)], pair_rs.at[which, c])
+        for m in (2 * c, 2 * c + 1):
+            both = pair_s[which, m] + pair_r[which, m ^ 1]
+            turned[which, :, m * toks : (m + 1) * toks] = both.T.astype(BF16)
+            if which == 0:
+                dq_p[m] = both
 
     for c in range(pairs):
         x = chunk(qg_a, c)
@@ -275,29 +292,11 @@
         grads = dot(
             jnp.concatenate([high, rest], axis=1), jnp.concatenate([st_high, st_high], axis=0)
         ) + dot(high, st_low)
-        out = feature_grad(x, feat_q[c] * grads)
-        placed = jnp.where(first, out, swap(out))
-        pq_s[2 * c] = placed[:toks]
-        pq_s[2 * c + 1] = placed[toks:]
-        pair_copy(0, pq_s, pq_r, c)
-
-    def give_back(which, sent, got):
-        for m in range(2, groups, 2):
-            remote(
-                sent.at[m], got.at[pair], back_ss.at[which], back_rs.at[which], flipped(me, m)
-            ).start()
-        got[pair] = sent[0]
-
-    def given_back(which, got):
-        settle(got.at[pl.ds(0, pairs - 1)], back_rs.at[which])
+        pair_send(0, c, feature_grad(x, feat_q[c] * grads, mine))
 
     relay(1)
     for c in range(pairs):
-        paired(0, pq_r, c)
-        for m in (2 * c, 2 * c + 1):
-            both = pq_s[m] + pq_r[m ^ 1]
-            dq_p[m] = both
-            turned[0, :, m * toks : (m + 1) * toks] = both.T.astype(BF16)
+        paired(0, c)
 
     def weight_part(which, q, rows):
         total = dot(turned[which], rows).T
@@ -327,44 +326,43 @@
     relay(2)
     weight_part(0, 0, hidden_rows(0))
 
-    gs_high, gs_low = finish(reduce_q)
+    total = finish(reduce_q)
+    states[mine] = total
+
+    def state_send(to, slot, which):
+        remote(states.at[slot], states.at[slot], st_ss.at[0], st_rs.at[which], to).start()
+
     weight_sends(0, 0)
+
+    def value_rows(x):
+        lane = lax.broadcasted_iota(jnp.int32, x.shape, 1)
+        ones = jnp.where(lane == head_dim - 1, 1.0, 0.0)
+        xv = jnp.where(low(x.shape), ones, x).astype(BF16)
+        return jnp.concatenate([xv, xv], axis=1)
+
+    gs_high, gs_low = spread(total)
     gs_both = jnp.concatenate([gs_high, gs_low], axis=0)
     for c in range(pairs):
         x = chunk(kv_a, c)
-        mask = low(x.shape)
-        lane = lax.broadcasted_iota(jnp.int32, x.shape, 1)
-        xv = jnp.where(mask, jnp.where(lane == head_dim - 1, 1.0, 0.0), x).astype(BF16)
-        b = feat_k[c]
-        grads = dot(jnp.concatenate([xv, xv], axis=1), gs_both)
-        out = feature_grad(x, b * grads)
-        high, rest = halves(b)
-        gv = dot_t(high, gs_both)
-        gv = gv[:, :LANES] + gv[:, LANES:] + dot_t(rest, gs_high)
-        packed = jnp.where(mask, out, gv)
-        pk_s[2 * c] = packed[:toks]
-        pk_s[2 * c + 1] = packed[toks:]
-        pair_copy(1, pk_s, pk_r, c)
+        grads = dot(value_rows(x), gs_both)
+        pair_send(1, c, feature_grad(x, feat_k[c] * grads, mine))
         if c == pairs // 2 - 1:
             relay(3)
+    for m in range(2, groups, 2):
+        state_send(flipped(me, m), mine, 0)
+    state_send(partner, mine, 1)
     weight_part(0, 1, hidden_rows(1))
     weight_sends(0, 1)
     for c in range(pairs):
-        paired(1, pk_r, c)
-        for m in (2 * c, 2 * c + 1):
-            own, theirs = pk_s[m], pk_r[m ^ 1]
-            one = jnp.where(first, own, theirs)
-            two = jnp.where(first, theirs, own)
-            mask = low(own.shape)
-            both = jnp.where(mask, one, swap(two))
-            dk_p[m] = both
-            turned[1, :, m * toks : (m + 1) * toks] = both.T.astype(BF16)
-            gv_p[m] = jnp.where(mask, swap(one), two)
+        paired(1, c)
+    for m in range(2, groups, 2):
+        remote(
+            dq_p.at[m], dq_a.at[pair], back_ss.at[0], back_rs.at[0], flipped(me, m)
+        ).start()
+    dq_a[pair] = dq_p[0]
     for q in range(2):
         weight_part(1, q, hid_r[q].reshape(groups * toks, LANES).astype(BF16))
         weight_sends(1, q)
-    give_back(0, dq_p, dq_a)
-    give_back(1, dk_p, dk_a)
     for q in range(2, parts):
         if q > 2:
             relay(q + 1)
@@ -372,17 +370,33 @@
         for which in range(2):
             weight_part(which, q, rows)
             weight_sends(which, q)
-    give_back(2, gv_p, gv_a)
-
-    def joined(ref):
-        return jnp.concatenate([ref[p] for p in range(pairs)], axis=1).astype(BF16)
-
-    given_back(0, dq_a)
-    o_hid[...] = dot_t(joined(dq_a), wq[...])
-    given_back(1, dk_a)
-    o_hid[...] += dot_t(joined(dk_a), wk[...])
-    given_back(2, gv_a)
-    o_val[...] = joined(gv_a)
+
+    if pairs > 1:
+        settle(states.at[pl.ds(0, pairs - 1)], st_rs.at[0])
+    for m in range(2, groups, 2):
+        state_send(partner, flipped(me, m) % groups, 1)
+    settle(states.at[pl.ds(0, pairs)], st_rs.at[1])
+    dk_slabs = []
+    for p in range(pairs):
+        outs = []
+        for j in (2 * p, 2 * p + 1):
+            gs_high, gs_low = spread(states[j])
+            gs_both = jnp.concatenate([gs_high, gs_low], axis=0)
+            x, b = kv_s[j], feat_l[j]
+            out = feature_grad(x, b * dot(value_rows(x), gs_both), j)
+            high, rest = halves(b)
+            gv = dot_t(high, gs_both)
+            gv = gv[:, :LANES] + gv[:, LANES:] + dot_t(rest, gs_high)
+            outs.append((out, gv))
+        (dk_one, gv_one), (dk_two, gv_two) = outs
+        mask = low(dk_one.shape)
+        dk_slabs.append(jnp.where(mask, dk_one, swap(dk_two)))
+        slab = jnp.where(mask, swap(gv_one), gv_two)
+        o_val[:, p * LANES : (p + 1) * LANES] = slab.astype(BF16)
+    o_hid[...] = dot_t(jnp.concatenate(dk_slabs, axis=1).astype(BF16), wk[...])
+    settle(dq_a.at[pl.ds(0, pairs - 1)], back_rs.at[0])
+    dq_all = jnp.concatenate([dq_a[p] for p in range(pairs)], axis=1).astype(BF16)
+    o_hid[...] += dot_t(dq_all, wq[...])
 
     for which in range(2):
         settle(gw_r.at[which], gw_rs.at[which])
@@ -395,7 +409,7 @@
     for which in range(2):
         others = kv_a.at[pl.ds(1, groups - 1)]
         settle(others, a2a_ss.at[which])
-        settle(pk_s, pair_ss.at[which])
+        settle(pair_s.at[which], pair_ss.at[which])
         own_set = me // (n // 2) == core
 
         @pl.when(own_set)
@@ -406,8 +420,8 @@
         def _():
             settle(gw_s.at[which], gw_ss.at[which])
 
-    for which in range(3):
-        settle(dq_a.at[pl.ds(0, pairs - 1)], back_ss.at[which])
+    settle(dq_a.at[pl.ds(0, pairs - 1)], back_ss.at[0])
+    settle(states.at[pl.ds(0, groups - 1)], st_ss.at[0])
     settle(hid_r.at[:, pl.ds(1, groups - 1)], hid_ss.at[0])
 
 
@@ -434,7 +448,6 @@
     phases = len(radices(n // groups))
     rows = head_dim + 8
     tok_block = (groups, toks, LANES)
-    own_block = (pairs, toks, LANES)
     scratch = [pltpu.VMEM(a.shape, a.dtype) for a in args]
     scratch += [
         pltpu.VMEM((2, parts, toks, LANES), F32),
@@ -442,21 +455,26 @@
     ]
     scratch += [pltpu.VMEM(tok_block, F32)] * 4
     scratch += [
-        pltpu.VMEM((4 * head_dim, feats), BF16),
-        pltpu.VMEM((2 * head_dim, feats), BF16),
+        pltpu.VMEM((groups, 4 * head_dim, feats), BF16),
+        pltpu.VMEM((groups, 2 * head_dim, feats), BF16),
         pltpu.VMEM((pairs, 2 * toks, feats), F32),
         pltpu.VMEM((pairs, 2 * toks, feats), F32),
         pltpu.VMEM((pairs, 2 * toks, LANES), F32),
         pltpu.VMEM((2, phases, rows, feats), F32),
         pltpu.VMEM((2, phases, 3, rows, feats), F32),
     ]
-    scratch += [pltpu.VMEM(tok_block, F32)] * 7
-    scratch += [pltpu.VMEM((2, LANES, groups * toks), BF16)]
-    scratch += [pltpu.VMEM(own_block, F32)] * 3
+    scratch += [pltpu.VMEM((2,) + tok_block, F32)] * 2
+    scratch += [
+        pltpu.VMEM(tok_block, F32),
+        pltpu.VMEM((2, LANES, groups * toks), BF16),
+        pltpu.VMEM((groups, toks, feats), F32),
+        pltpu.VMEM((groups, rows, feats), F32),
+        pltpu.VMEM((pairs, toks, LANES), F32),
+    ]
     scratch += [pltpu.VMEM((2, n // 2, block, LANES), F32)] * 2
     for shape in (
         (6,), (2,), (2, pairs), (1,), (parts, 2), (2, phases), (2, phases), (2,), (2, pairs),
-        (3,), (3,), (2,), (2,),
+        (1,), (1,), (1,), (2,), (2,), (2,),
     ):
         scratch.append(pltpu.SemaphoreType.DMA(shape))
     vmem = pl.BlockSpec(memory_space=pltpu.VMEM)

time: 54.7 us -> 51.2 us (0.936)
  the two profiles are of different devices: /device:TPU:8 before, /device:TPU:0 now
where the time goes in v4:
time: 51.2 us; the launch traced here: 50.3 us
  Pallas kernels  49.6 us (97%)
  between operations  0.64 us (1%)
    pallas_call x1, Pallas kernels, shards(): pl.pallas_call(functools.partial(kernel, n), out_shape=tuple((pltpu.VMEM(...  48.7 us

profile of v4, /device:TPU:0, one launch (start us, length us, event | category | flops | bytes accessed | tf_op | source)
XLA Modules:
  0.0 50.3 jit_solution(5996575989706990260)
XLA Ops:
  0.6 48.7 %backward.1 = (f32[128,1024]{1,0:T(8,128)S(1)}, bf16[128,512]{1,0:T(8,128)(2,1)S(1)}, f32[32,512]{1,0:T(8,128)S(1)}, f32[32,512]{1,0:T(8,128)S(1)}) custom-call(bf16[128,1024]{1,0:T(8,128)(2,1)} %hid_h.1, bf16[1024,512]{1,0:T(8,128)(2,1)} %wq_h.1, bf16[1024,512]{1,0:T(8,128)(2,1)} %wk_h.1, bf16[128,512]{1,0:T(8,128)(2,1)} %val_h.1, bf16[128,512]{1,0:T(8,128)(2,1)} %gout_h.1, ...), custom_call_target="tpu_custom_call" | custom-call | tf_op jit(solution)/shard_map/backward/pallas_call | solution.py:488
  49.4 0.9 %store.1 = (f32[128,1024]{1,0:T(8,128)}, bf16[128,512]{1,0:T(8,128)(2,1)}, f32[32,512]{1,0:T(8,128)}, f32[32,512]{1,0:T(8,128)}) custom-call(f32[128,1024]{1,0:T(8,128)S(1)} %get-tuple-element.8.refs_0_, bf16[128,512]{1,0:T(8,128)(2,1)S(1)} %get-tuple-element.9.refs_1_, f32[32,512]{1,0:T(8,128)S(1)} %get-tuple-element.10.refs_2_, ...), custom_call_target="tpu_custom_call" | custom-call | tf_op jit(solution)/shard_map/store/pallas_call | solution.py:499

commit v5 on v4

--- a/solution.py
+++ b/solution.py
@@ -62,16 +62,17 @@
     n, hid_h, wq_h, wk_h, val_h, gout_h, rf_h, o_hid, o_val, o_gq, o_gk,
     hid, wq, wk, val, gout, rf,
     hid_f, hid_r, kv_s, kv_a, qg_s, qg_a, rfs, rbs, feat_k, feat_q, bwd_x,
-    ar_s, ar_r, pair_s, pair_r, dq_p, turned, feat_l, states, dq_a, gw_s, gw_r,
+    ar_s, ar_r, pair_s, pair_r, dq_p, turned, feat_l, states, dq_a, gw_s, gw_x, gw_r,
     in_ss, a2a_ss, a2a_rs, hid_ss, hid_rs, ar_ss, ar_rs, pair_ss, pair_rs, back_ss, back_rs,
-    st_ss, st_rs, gw_ss, gw_rs,
+    st_ss, st_rs, gw_ss, gw_xs, gw_rs,
 ):
     groups, head_dim, feats = rf.shape
     toks, width = hid.shape
     half = width // 2
     parts = half // LANES
-    block = gw_s.shape[2]
+    block = gw_s.shape[3]
     per = LANES // block
+    later = parts // 2
     pairs = groups // 2
     scale = head_dim ** (-0.25)
     norm = feats ** (-0.5)
@@ -82,6 +83,9 @@
     first = core == 0
     phases = radices(n // groups)
     partner = flipped(me, 1)
+    parity = (me // groups) % 2
+    plane_next = flipped(me, 1, groups)
+    order = [(i + (1 - parity) * later) % parts for i in range(parts)]
 
     barrier = pltpu.get_barrier_semaphore()
 
@@ -91,13 +95,14 @@
         )
         return carry
 
-    lax.fori_loop(1, n, greet, 0)
     loads = []
     for i, (src, dst) in enumerate(
         [(hid_h, hid), (wk_h, wk), (val_h, val), (wq_h, wq), (gout_h, gout), (rf_h, rf)]
     ):
         loads.append(pltpu.make_async_copy(src, dst, in_ss.at[i]))
-        loads[-1].start()
+    for load in loads[:3]:
+        load.start()
+    lax.fori_loop(1, n, greet, 0)
 
     def low(shape):
         return lax.broadcasted_iota(jnp.int32, shape, 1) < head_dim
@@ -124,6 +129,8 @@
 
     for load in loads[:3]:
         load.wait()
+    for load in loads[3:]:
+        load.start()
     pack(dot(hid[...], wk[...]) * scale, val[...], kv_s)
     pl.semaphore_wait(barrier, n - 1)
     scatter(0, kv_s, kv_a)
@@ -134,8 +141,8 @@
 
     for h in range(2):
         for q in range(parts):
-            spot = h * half + q * LANES
-            hid_f[h, q] = hid[:, spot : spot + LANES].astype(F32)
+            spot = pl.multiple_of(h * half + order[q] * LANES, LANES)
+            hid_f[h, q] = hid[:, pl.ds(spot, LANES)].astype(F32)
 
     relayed = [m for m in range(1, groups) if m & 6 == 6 and m < 8]
     direct = [m for m in range(1, groups) if m not in relayed]
@@ -268,60 +275,70 @@
         out = (back - x * jnp.sum(weighted, axis=1, keepdims=True)) * scale
         return jnp.where(low(x.shape), out.astype(BF16).astype(F32), 0.0)
 
-    def pair_send(which, c, out):
-        placed = jnp.where(first, out, swap(out))
-        pair_s[which, 2 * c] = placed[:toks]
-        pair_s[which, 2 * c + 1] = placed[toks:]
-        two = pl.ds(2 * c, 2)
-        remote(
-            pair_s.at[which, two], pair_r.at[which, two],
-            pair_ss.at[which], pair_rs.at[which, c], partner,
-        ).start()
+    def pair_send(which, outs):
+        for c, out in outs:
+            pair_s[which, c] = out[:toks] + swap(out[toks:])
+        for c, _ in outs:
+            remote(
+                pair_s.at[which, c], pair_r.at[which, c],
+                pair_ss.at[which], pair_rs.at[which, c], partner,
+            ).start()
 
     def paired(which, c):
-        settle(pair_r.at[which, pl.ds(2 * c, 2)], pair_rs.at[which, c])
-        for m in (2 * c, 2 * c + 1):
-            both = pair_s[which, m] + pair_r[which, m ^ 1]
+        settle(pair_r.at[which, c], pair_rs.at[which, c])
+        own, theirs = pair_s[which, c], pair_r[which, c]
+        mask = low(own.shape)
+        for m, a, b in ((2 * c, own, swap(theirs)), (2 * c + 1, swap(own), theirs)):
+            both = jnp.where(first, jnp.where(mask, a, swap(b)), jnp.where(mask, b, swap(a)))
             turned[which, :, m * toks : (m + 1) * toks] = both.T.astype(BF16)
             if which == 0:
                 dq_p[m] = both
 
-    for c in range(pairs):
+    def query_grad(c):
         x = chunk(qg_a, c)
         high, rest = halves(bwd_x[c])
         grads = dot(
             jnp.concatenate([high, rest], axis=1), jnp.concatenate([st_high, st_high], axis=0)
         ) + dot(high, st_low)
-        pair_send(0, c, feature_grad(x, feat_q[c] * grads, mine))
+        return c, feature_grad(x, feat_q[c] * grads, mine)
+
+    for c in range(0, pairs, 2):
+        pair_send(0, [query_grad(c), query_grad(c + 1)])
 
     relay(1)
     for c in range(pairs):
         paired(0, c)
 
     def weight_part(which, q, rows):
-        total = dot(turned[which], rows).T
-        gw_s[which, q * per : (q + 1) * per] = total.reshape(per, block, LANES)
-
-    def weight_sends(which, q):
+        total = dot(turned[which], rows).T.reshape(per, block, LANES)
+        if q < later:
+            gw_s[which, q] = total
+            remote(
+                gw_s.at[which, q], gw_x.at[which, q], gw_ss.at[2], gw_xs.at[which, q], plane_next
+            ).start()
+            return
+        settle(gw_x.at[which, q - later], gw_xs.at[which, q - later])
+        gw_s[which, q] = total + gw_x[which, q - later]
+        slot = (me // groups) // 2 * pairs + pair
+
         def start(i, carry):
-            to = core * (n // 2) + i
+            to = core * (n // 2) + order[q] * per + i
 
             @pl.when(to != me)
             def _():
                 remote(
-                    gw_s.at[which, i], gw_r.at[which, me // 2],
-                    gw_ss.at[which], gw_rs.at[which], to,
+                    gw_s.at[which, q, i], gw_r.at[which, slot], gw_ss.at[which], gw_rs.at[which], to
                 ).start()
 
             @pl.when(to == me)
             def _():
                 pltpu.make_async_copy(
-                    gw_s.at[which, i], gw_r.at[which, me // 2], gw_rs.at[which]
+                    gw_s.at[which, q, i], gw_r.at[which, slot], gw_rs.at[which]
                 ).start()
 
             return carry
 
-        lax.fori_loop(q * per, (q + 1) * per, start, 0)
+        lax.fori_loop(0, per, start, 0)
 
     relay(2)
     weight_part(0, 0, hidden_rows(0))
@@ -332,7 +349,6 @@
     def state_send(to, slot, which):
         remote(states.at[slot], states.at[slot], st_ss.at[0], st_rs.at[which], to).start()
 
-    weight_sends(0, 0)
 
     def value_rows(x):
         lane = lax.broadcasted_iota(jnp.int32, x.shape, 1)
@@ -342,17 +358,19 @@
 
     gs_high, gs_low = spread(total)
     gs_both = jnp.concatenate([gs_high, gs_low], axis=0)
-    for c in range(pairs):
+
+    def key_grad(c):
         x = chunk(kv_a, c)
-        grads = dot(value_rows(x), gs_both)
-        pair_send(1, c, feature_grad(x, feat_k[c] * grads, mine))
-        if c == pairs // 2 - 1:
+        return c, feature_grad(x, feat_k[c] * dot(value_rows(x), gs_both), mine)
+
+    for c in range(0, pairs, 2):
+        pair_send(1, [key_grad(c), key_grad(c + 1)])
+        if c == 0:
             relay(3)
     for m in range(2, groups, 2):
         state_send(flipped(me, m), mine, 0)
     state_send(partner, mine, 1)
     weight_part(0, 1, hidden_rows(1))
-    weight_sends(0, 1)
     for c in range(pairs):
         paired(1, c)
     for m in range(2, groups, 2):
@@ -362,14 +380,12 @@
     dq_a[pair] = dq_p[0]
     for q in range(2):
         weight_part(1, q, hid_r[q].reshape(groups * toks, LANES).astype(BF16))
-        weight_sends(1, q)
     for q in range(2, parts):
         if q > 2:
             relay(q + 1)
         rows = hidden_rows(q)
         for which in range(2):
             weight_part(which, q, rows)
-            weight_sends(which, q)
 
     if pairs > 1:
         settle(states.at[pl.ds(0, pairs - 1)], st_rs.at[0])
@@ -403,23 +419,24 @@
     for which, out in ((0, o_gq), (1, o_gk)):
         for p in range(pairs):
             total = gw_r[which, p]
-            for i in range(p + pairs, n // 2, pairs):
+            for i in range(p + pairs, n // 4, pairs):
                 total = total + gw_r[which, i]
             out[:, p * LANES : (p + 1) * LANES] = total
     for which in range(2):
         others = kv_a.at[pl.ds(1, groups - 1)]
         settle(others, a2a_ss.at[which])
         settle(pair_s.at[which], pair_ss.at[which])
-        own_set = me // (n // 2) == core
+        own_set = me // (n // 4) == 2 * core + parity
 
         @pl.when(own_set)
         def _():
-            settle(gw_s.at[which, pl.ds(0, n // 2 - 1)], gw_ss.at[which])
+            settle(gw_r.at[which, pl.ds(0, n // 4 - 1)], gw_ss.at[which])
 
         @pl.when(jnp.logical_not(own_set))
         def _():
-            settle(gw_s.at[which], gw_ss.at[which])
-
+            settle(gw_r.at[which], gw_ss.at[which])
+
+    settle(gw_x, gw_ss.at[2])
     settle(dq_a.at[pl.ds(0, pairs - 1)], back_ss.at[0])
     settle(states.at[pl.ds(0, groups - 1)], st_ss.at[0])
     settle(hid_r.at[:, pl.ds(1, groups - 1)], hid_ss.at[0])
@@ -463,7 +480,7 @@
         pltpu.VMEM((2, phases, rows, feats), F32),
         pltpu.VMEM((2, phases, 3, rows, feats), F32),
     ]
-    scratch += [pltpu.VMEM((2,) + tok_block, F32)] * 2
+    scratch += [pltpu.VMEM((2, pairs, toks, LANES), F32)] * 2
     scratch += [
         pltpu.VMEM(tok_block, F32),
         pltpu.VMEM((2, LANES, groups * toks), BF16),
@@ -471,10 +488,14 @@
         pltpu.VMEM((groups, rows, feats), F32),
         pltpu.VMEM((pairs, toks, LANES), F32),
     ]
-    scratch += [pltpu.VMEM((2, n // 2, block, LANES), F32)] * 2
+    scratch += [
+        pltpu.VMEM((2, parts, LANES // block, block, LANES), F32),
+        pltpu.VMEM((2, parts // 2, LANES // block, block, LANES), F32),
+        pltpu.VMEM((2, n // 4, block, LANES), F32),
+    ]
     for shape in (
         (6,), (2,), (2, pairs), (1,), (parts, 2), (2, phases), (2, phases), (2,), (2, pairs),
-        (1,), (1,), (1,), (2,), (2,), (2,),
+        (1,), (1,), (1,), (2,), (3,), (2, parts // 2), (2,),
     ):
         scratch.append(pltpu.SemaphoreType.DMA(shape))
     vmem = pl.BlockSpec(memory_space=pltpu.VMEM)

time: 51.2 us -> 47.5 us (0.928); the launches traced: 50.3 us -> 47.4 us
  Pallas kernels: 49.6 us -> 46.7 us
    pallas_call x1, Pallas kernels: 48.7 us -> 45.8 us  [shards(): pl.pallas_call(functools.partial(kernel, n), out_shape=tuple((pltpu.VMEM(...]
where the time goes in v5:
time: 47.5 us; the launch traced here: 47.4 us
  Pallas kernels  46.7 us (98%)
  between operations  0.64 us (1%)
    pallas_call x1, Pallas kernels, shards(): pl.pallas_call(functools.partial(kernel, n), out_shape=tuple((pltpu.VMEM(...  45.8 us

profile of v5, /device:TPU:0, one launch (start us, length us, event | category | flops | bytes accessed | tf_op | source)
XLA Modules:
  0.0 47.4 jit_solution(6691727715155085735)
XLA Ops:
  0.6 45.8 %backward.1 = (f32[128,1024]{1,0:T(8,128)S(1)}, bf16[128,512]{1,0:T(8,128)(2,1)S(1)}, f32[32,512]{1,0:T(8,128)S(1)}, f32[32,512]{1,0:T(8,128)S(1)}) custom-call(bf16[128,1024]{1,0:T(8,128)(2,1)} %hid_h.1, bf16[1024,512]{1,0:T(8,128)(2,1)} %wq_h.1, bf16[1024,512]{1,0:T(8,128)(2,1)} %wk_h.1, bf16[128,512]{1,0:T(8,128)(2,1)} %val_h.1, bf16[128,512]{1,0:T(8,128)(2,1)} %gout_h.1, ...), custom_call_target="tpu_custom_call" | custom-call | tf_op jit(solution)/shard_map/backward/pallas_call | solution.py:509
  46.5 0.9 %store.1 = (f32[128,1024]{1,0:T(8,128)}, bf16[128,512]{1,0:T(8,128)(2,1)}, f32[32,512]{1,0:T(8,128)}, f32[32,512]{1,0:T(8,128)}) custom-call(f32[128,1024]{1,0:T(8,128)S(1)} %get-tuple-element.8.refs_0_, bf16[128,512]{1,0:T(8,128)(2,1)S(1)} %get-tuple-element.9.refs_1_, f32[32,512]{1,0:T(8,128)S(1)} %get-tuple-element.10.refs_2_, ...), custom_call_target="tpu_custom_call" | custom-call | tf_op jit(solution)/shard_map/store/pallas_call | solution.py:520

commit v6 on v5

--- a/solution.py
+++ b/solution.py
@@ -61,7 +61,7 @@
 def kernel(
     n, hid_h, wq_h, wk_h, val_h, gout_h, rf_h, o_hid, o_val, o_gq, o_gk,
     hid, wq, wk, val, gout, rf,
-    hid_f, hid_r, kv_s, kv_a, qg_s, qg_a, rfs, rbs, feat_k, feat_q, bwd_x,
+    hid_f, hid_r, kv_s, kv_a, qg_s, qg_a, rfs, rbs, feat_k, feat_q, feat_h, bwd_x,
     ar_s, ar_r, pair_s, pair_r, dq_p, turned, feat_l, states, dq_a, gw_s, gw_x, gw_r,
     in_ss, a2a_ss, a2a_rs, hid_ss, hid_rs, ar_ss, ar_rs, pair_ss, pair_rs, back_ss, back_rs,
     st_ss, st_rs, gw_ss, gw_xs, gw_rs,
@@ -147,7 +147,7 @@
     relayed = [m for m in range(1, groups) if m & 6 == 6 and m < 8]
     direct = [m for m in range(1, groups) if m not in relayed]
     passed_on = [2, 5] if relayed else []
-    ahead = 3
+    ahead = 2
 
     def hidden_start(q, m):
         if m in relayed:
@@ -196,10 +196,26 @@
     def chunk(ref, c):
         return ref[2 * c : 2 * c + 2].reshape(2 * toks, ref.shape[2])
 
+    def folded(total):
+        slabs = [total[:, s : s + LANES] for s in range(0, feats, LANES)]
+        return jnp.concatenate([t[head_dim:] for t in slabs] + [t[:1] for t in slabs], axis=0)
+
+    def spread(packed):
+        count = feats // LANES
+        rows = jnp.concatenate(
+            [packed[i * head_dim : (i + 1) * head_dim] for i in range(count)], axis=1
+        )
+        base = count * head_dim
+        z = jnp.concatenate([packed[base + i : base + i + 1] for i in range(count)], axis=1)
+        return halves(
+            jnp.concatenate([jnp.broadcast_to(z, (head_dim, feats)), rows], axis=0)
+        )
+
     def all_reduce(which, total):
+        packed = folded(total)
         stride = groups
         for f, radix in enumerate(phases):
-            ar_s[which, f] = total
+            ar_s[which, f] = packed
             for d in range(1, radix):
                 remote(
                     ar_s.at[which, f], ar_r.at[which, f, d - 1],
@@ -210,23 +226,14 @@
             settle(came, ar_rs.at[which, f])
             settle(came, ar_ss.at[which, f])
             for d in range(radix - 1):
-                total = total + ar_r[which, f, d]
+                packed = packed + ar_r[which, f, d]
             stride *= radix
-        yield total
+        yield packed
 
     def finish(steps):
         for got in steps:
             if got is not None:
                 return got
-
-    def spread(total):
-        return halves(
-            jnp.concatenate(
-                [jnp.broadcast_to(total[7:8], (head_dim, feats)), total[8:]], axis=0
-            )
-        )
-
-    lead = head_dim - 8
 
     for j in range(groups):
         feat_l[j] = features(kv_s[j], j)
@@ -240,31 +247,33 @@
         high, rest = halves(b)
         ones = jnp.where(low(x.shape), 1.0, x).T.astype(BF16)
         total = total + dot(ones, high) + dot(ones, rest)
-    reduce_k = all_reduce(0, total[lead:])
+    reduce_k = all_reduce(0, total)
     next(reduce_k)
 
     for c in range(pairs):
         scattered(1, qg_a, c)
-        feat_q[c] = features(chunk(qg_a, c), mine)
+        a = features(chunk(qg_a, c), mine)
+        feat_q[c] = a
+        feat_h[0, c], feat_h[1, c] = halves(a)
 
     st_high, st_low = spread(finish(reduce_k))
     st_both = jnp.concatenate([st_high, st_low], axis=0)
     total = jnp.zeros((LANES, feats), F32)
     for c in range(pairs):
         x = chunk(qg_a, c)
-        high, rest = halves(feat_q[c])
+        high, rest = feat_h[0, c], feat_h[1, c]
         nd = dot_t(high, st_both)
         nd = nd[:, :LANES] + nd[:, LANES:] + dot_t(rest, st_high)
         mask = low(nd.shape)
-        den = jnp.where(mask, nd, swap(nd))
-        upstream = jnp.where(mask, 0.0, x) / den
-        grad_den = -jnp.sum(upstream * nd / den, axis=1, keepdims=True)
+        inverse = 1.0 / jnp.where(mask, nd, swap(nd))
+        upstream = jnp.where(mask, 0.0, x) * inverse
+        grad_den = -jnp.sum(upstream * (nd * inverse), axis=1, keepdims=True)
         lane = lax.broadcasted_iota(jnp.int32, nd.shape, 1)
-        xg = jnp.where(lane == head_dim - 1, grad_den, upstream)
+        xg = jnp.where(lane == 0, grad_den, upstream)
         bwd_x[c] = xg
         turned_high, turned_low = halves(xg.T)
         total = total + dot(turned_high, high) + dot(turned_low, high) + dot(turned_high, rest)
-    reduce_q = all_reduce(1, total[lead:])
+    reduce_q = all_reduce(1, total)
     next(reduce_q)
     relay(0)
 
@@ -352,7 +361,7 @@
 
     def value_rows(x):
         lane = lax.broadcasted_iota(jnp.int32, x.shape, 1)
-        ones = jnp.where(lane == head_dim - 1, 1.0, 0.0)
+        ones = jnp.where(lane == 0, 1.0, 0.0)
         xv = jnp.where(low(x.shape), ones, x).astype(BF16)
         return jnp.concatenate([xv, xv], axis=1)
 
@@ -365,27 +374,26 @@
 
     for c in range(0, pairs, 2):
         pair_send(1, [key_grad(c), key_grad(c + 1)])
-        if c == 0:
-            relay(3)
+    relay(3)
     for m in range(2, groups, 2):
         state_send(flipped(me, m), mine, 0)
     state_send(partner, mine, 1)
     weight_part(0, 1, hidden_rows(1))
     for c in range(pairs):
         paired(1, c)
+    for q in range(later):
+        weight_part(1, q, hid_r[q].reshape(groups * toks, LANES).astype(BF16))
     for m in range(2, groups, 2):
         remote(
             dq_p.at[m], dq_a.at[pair], back_ss.at[0], back_rs.at[0], flipped(me, m)
         ).start()
     dq_a[pair] = dq_p[0]
-    for q in range(2):
-        weight_part(1, q, hid_r[q].reshape(groups * toks, LANES).astype(BF16))
-    for q in range(2, parts):
+    for q in range(later, parts):
         if q > 2:
             relay(q + 1)
-        rows = hidden_rows(q)
-        for which in range(2):
-            weight_part(which, q, rows)
+        weight_part(0, q, hidden_rows(q))
+    for q in range(later, parts):
+        weight_part(1, q, hid_r[q].reshape(groups * toks, LANES).astype(BF16))
 
     if pairs > 1:
         settle(states.at[pl.ds(0, pairs - 1)], st_rs.at[0])
@@ -463,7 +471,7 @@
     block = width // n
     parts = width // 2 // LANES
     phases = len(radices(n // groups))
-    rows = head_dim + 8
+    rows = (head_dim + 1) * feats // LANES
     tok_block = (groups, toks, LANES)
     scratch = [pltpu.VMEM(a.shape, a.dtype) for a in args]
     scratch += [
@@ -476,16 +484,17 @@
         pltpu.VMEM((groups, 2 * head_dim, feats), BF16),
         pltpu.VMEM((pairs, 2 * toks, feats), F32),
         pltpu.VMEM((pairs, 2 * toks, feats), F32),
+        pltpu.VMEM((2, pairs, 2 * toks, feats), BF16),
         pltpu.VMEM((pairs, 2 * toks, LANES), F32),
-        pltpu.VMEM((2, phases, rows, feats), F32),
-        pltpu.VMEM((2, phases, 3, rows, feats), F32),
+        pltpu.VMEM((2, phases, rows, LANES), F32),
+        pltpu.VMEM((2, phases, 3, rows, LANES), F32),
     ]
     scratch += [pltpu.VMEM((2, pairs, toks, LANES), F32)] * 2
     scratch += [
         pltpu.VMEM(tok_block, F32),
         pltpu.VMEM((2, LANES, groups * toks), BF16),
         pltpu.VMEM((groups, toks, feats), F32),
-        pltpu.VMEM((groups, rows, feats), F32),
+        pltpu.VMEM((groups, rows, LANES), F32),
         pltpu.VMEM((pairs, toks, LANES), F32),
     ]
     scratch += [

time: 47.5 us -> 47.2 us (level)
  no operation moved by 1% of the time
where the time goes in v6:
time: 47.2 us; the launch traced here: 47 us
  Pallas kernels  46.4 us (98%)
  between operations  0.64 us (1%)
    pallas_call x1, Pallas kernels, shards(): pl.pallas_call(functools.partial(kernel, n), out_shape=tuple((pltpu.VMEM(...  45.5 us

profile of v6, /device:TPU:0, one launch (start us, length us, event | category | flops | bytes accessed | tf_op | source)
XLA Modules:
  0.0 47.0 jit_solution(11858469560997448576)
XLA Ops:
  0.6 45.5 %backward.1 = (f32[128,1024]{1,0:T(8,128)S(1)}, bf16[128,512]{1,0:T(8,128)(2,1)S(1)}, f32[32,512]{1,0:T(8,128)S(1)}, f32[32,512]{1,0:T(8,128)S(1)}) custom-call(bf16[128,1024]{1,0:T(8,128)(2,1)} %hid_h.1, bf16[1024,512]{1,0:T(8,128)(2,1)} %wq_h.1, bf16[1024,512]{1,0:T(8,128)(2,1)} %wk_h.1, bf16[128,512]{1,0:T(8,128)(2,1)} %val_h.1, bf16[128,512]{1,0:T(8,128)(2,1)} %gout_h.1, ...), custom_call_target="tpu_custom_call" | custom-call | tf_op jit(solution)/shard_map/backward/pallas_call | solution.py:518
  46.1 0.9 %store.1 = (f32[128,1024]{1,0:T(8,128)}, bf16[128,512]{1,0:T(8,128)(2,1)}, f32[32,512]{1,0:T(8,128)}, f32[32,512]{1,0:T(8,128)}) custom-call(f32[128,1024]{1,0:T(8,128)S(1)} %get-tuple-element.8.refs_0_, bf16[128,512]{1,0:T(8,128)(2,1)S(1)} %get-tuple-element.9.refs_1_, f32[32,512]{1,0:T(8,128)S(1)} %get-tuple-element.10.refs_2_, ...), custom_call_target="tpu_custom_call" | custom-call | tf_op jit(solution)/shard_map/store/pallas_call | solution.py:529

commit v7 on v6

--- a/solution.py
+++ b/solution.py
@@ -147,7 +147,7 @@
     relayed = [m for m in range(1, groups) if m & 6 == 6 and m < 8]
     direct = [m for m in range(1, groups) if m not in relayed]
     passed_on = [2, 5] if relayed else []
-    ahead = 2
+    ahead = 3
 
     def hidden_start(q, m):
         if m in relayed:
@@ -399,21 +399,24 @@
         settle(states.at[pl.ds(0, pairs - 1)], st_rs.at[0])
     for m in range(2, groups, 2):
         state_send(partner, flipped(me, m) % groups, 1)
+
+    def own_grads(j):
+        gs_high, gs_low = spread(states[j])
+        gs_both = jnp.concatenate([gs_high, gs_low], axis=0)
+        x, b = kv_s[j], feat_l[j]
+        out = feature_grad(x, b * dot(value_rows(x), gs_both), j)
+        high, rest = halves(b)
+        gv = dot_t(high, gs_both)
+        return out, gv[:, :LANES] + gv[:, LANES:] + dot_t(rest, gs_high)
+
+    here = [own_grads(2 * p + core) for p in range(pairs)]
     settle(states.at[pl.ds(0, pairs)], st_rs.at[1])
+    there = [own_grads(2 * p + 1 - core) for p in range(pairs)]
     dk_slabs = []
-    for p in range(pairs):
-        outs = []
-        for j in (2 * p, 2 * p + 1):
-            gs_high, gs_low = spread(states[j])
-            gs_both = jnp.concatenate([gs_high, gs_low], axis=0)
-            x, b = kv_s[j], feat_l[j]
-            out = feature_grad(x, b * dot(value_rows(x), gs_both), j)
-            high, rest = halves(b)
-            gv = dot_t(high, gs_both)
-            gv = gv[:, :LANES] + gv[:, LANES:] + dot_t(rest, gs_high)
-            outs.append((out, gv))
-        (dk_one, gv_one), (dk_two, gv_two) = outs
-        mask = low(dk_one.shape)
+    for p, ((dk_own, gv_own), (dk_other, gv_other)) in enumerate(zip(here, there)):
+        mask = low(dk_own.shape)
+        dk_one, dk_two = jnp.where(first, dk_own, dk_other), jnp.where(first, dk_other, dk_own)
+        gv_one, gv_two = jnp.where(first, gv_own, gv_other), jnp.where(first, gv_other, gv_own)
         dk_slabs.append(jnp.where(mask, dk_one, swap(dk_two)))
         slab = jnp.where(mask, swap(gv_one), gv_two)
         o_val[:, p * LANES : (p + 1) * LANES] = slab.astype(BF16)

time: 47.2 us -> 47.2 us (level)
  no operation moved by 1% of the time
where the time goes in v7:
time: 47.2 us; the launch traced here: 47 us
  Pallas kernels  46.4 us (98%)
  between operations  0.64 us (1%)
    pallas_call x1, Pallas kernels, shards(): pl.pallas_call(functools.partial(kernel, n), out_shape=tuple((pltpu.VMEM(...  45.5 us

profile of v7, /device:TPU:0, one launch (start us, length us, event | category | flops | bytes accessed | tf_op | source)
XLA Modules:
  0.0 47.0 jit_solution(17328154057940154767)
XLA Ops:
  0.6 45.5 %backward.1 = (f32[128,1024]{1,0:T(8,128)S(1)}, bf16[128,512]{1,0:T(8,128)(2,1)S(1)}, f32[32,512]{1,0:T(8,128)S(1)}, f32[32,512]{1,0:T(8,128)S(1)}) custom-call(bf16[128,1024]{1,0:T(8,128)(2,1)} %hid_h.1, bf16[1024,512]{1,0:T(8,128)(2,1)} %wq_h.1, bf16[1024,512]{1,0:T(8,128)(2,1)} %wk_h.1, bf16[128,512]{1,0:T(8,128)(2,1)} %val_h.1, bf16[128,512]{1,0:T(8,128)(2,1)} %gout_h.1, ...), custom_call_target="tpu_custom_call" | custom-call | tf_op jit(solution)/shard_map/backward/pallas_call | solution.py:521
  46.1 0.9 %store.1 = (f32[128,1024]{1,0:T(8,128)}, bf16[128,512]{1,0:T(8,128)(2,1)}, f32[32,512]{1,0:T(8,128)}, f32[32,512]{1,0:T(8,128)}) custom-call(f32[128,1024]{1,0:T(8,128)S(1)} %get-tuple-element.8.refs_0_, bf16[128,512]{1,0:T(8,128)(2,1)S(1)} %get-tuple-element.9.refs_1_, f32[32,512]{1,0:T(8,128)S(1)} %get-tuple-element.10.refs_2_, ...), custom_call_target="tpu_custom_call" | custom-call | tf_op jit(solution)/shard_map/store/pallas_call | solution.py:532
